TPU v7x, 32 devices: a whole 2x2x4 slice. The times are simulated.
32 devices in a mesh: gx: 8 (over y, x, core), gy: 4 (over z).
Axes of the slice: x: 2, y: 2, z: 4, core: 2. Of those that a mesh axis runs over, the one named last changes fastest.
Arguments:
- nodes: bfloat16 [32768, 128], P(('gx', 'gy')), may hold values from -6 to 6
- ghost_rows: int32 [32, 8, 256], P(('gx', 'gy')), may hold values from 0 to 1023
- ghost_count: int32 [32, 8], P(('gx', 'gy')), may hold values from 0 to 256, as said below
- edge_send: int32 [32, 4096], P(('gx', 'gy')), may hold values from 0 to 3071
- edge_recv: int32 [32, 4096], P(('gx', 'gy')), may hold values from 0 to 1023
- edge_count: int32 [32], P(('gx', 'gy')), may hold values from 512 to 4096, as said below
- pool_map: int32 [32, 1024], P(('gx', 'gy')), may hold values from 0 to 191, as said below
- w_edge_in: bfloat16 [256, 128], replicated, may hold values from -0.375 to 0.375
- w_edge_out: bfloat16 [128, 128], replicated, may hold values from -0.5 to 0.5
- w_node_in: bfloat16 [256, 128], replicated, may hold values from -0.375 to 0.375
- w_node_out: bfloat16 [128, 128], replicated, may hold values from -0.5 to 0.5
- w_coarse_in: bfloat16 [128, 128], replicated, may hold values from -0.5 to 0.5
- w_coarse_out: bfloat16 [128, 128], replicated, may hold values from -0.5 to 0.5
- d_fine: bfloat16 [32768, 128], P(('gx', 'gy')), may hold values from -6 to 6
- d_coarse: bfloat16 [4096, 128], P(('gx', 'gy')), may hold values from -6 to 6
Outputs:
- fine_out: bfloat16 [32768, 128], P(('gx', 'gy'))
- coarse_out: bfloat16 [4096, 128], P(('gx', 'gy'))
- grad_nodes: float32 [32768, 128], P(('gx', 'gy'))
- grad_edge_in: float32 [256, 128], replicated
- grad_edge_out: float32 [128, 128], replicated
- grad_node_in: float32 [256, 128], replicated
- grad_node_out: float32 [128, 128], replicated
- grad_coarse_in: float32 [128, 128], replicated
- grad_coarse_out: float32 [128, 128], replicated
Inputs may be any that keep to these rules, and one draw needn't show every extreme that they name: `ghost_count`: every device fills all 256 slots for at least one offset. `edge_count`: at least one device has all 4096 slots live. `pool_map`: values under 32 occur only on devices that are not first along gy, and values of 160 or more only on devices that are not last along gy, so every parent lies in the device's gx column.
All inputs are finite; a program needn't handle non-finite values.
Results may differ from a plain program's by a relative error of at most 0.012.
Values may be sent and summed in bfloat16 or wider, within the bound.
A program may use at most 64 MiB of HBM per device.

v0:
```python
import functools

import jax
import jax.numpy as jnp
from jax import lax
from jax.experimental import pallas as pl
from jax.experimental.pallas import tpu as pltpu
from jax.sharding import PartitionSpec as P

BAND = 32
MESH = pl.DeviceIdType.MESH
ACROSS = (-1, -1, -1, 0, 0, 1, 1, 1)
ALONG = (-1, 0, 1, -1, 1, -1, 0, 1)
SEND_ORDER = (0, 2, 5, 7, 3, 4, 1, 6)
F32 = jnp.float32
BF16 = jnp.bfloat16
FOLDS = 4
LANES = 128


def mm(a, b):
    return jnp.dot(a, b, preferred_element_type=F32)


def mm_t(a, b):
    return lax.dot_general(a, b, (((1,), (1,)), ((), ())), preferred_element_type=F32)


def t_mm(a, b):
    return lax.dot_general(a, b, (((0,), (0,)), ((), ())), preferred_element_type=F32)


def sigmoid(v):
    return 1.0 / (1.0 + jnp.exp(-v))


def columns(row):
    return jnp.concatenate(
        [
            jnp.transpose(jnp.broadcast_to(row[:, s : s + LANES], (LANES, LANES)))
            for s in range(0, row.shape[1], LANES)
        ],
        axis=0,
    )


def alive(row, start, count):
    ids = lax.broadcasted_iota(jnp.int32, row.shape, 1) + start
    return jnp.where(ids < count, row, -1)


def pick_lanes(col, width):
    ids = lax.broadcasted_iota(jnp.int32, (col.shape[0], LANES), 1)
    parts = [
        jnp.where(ids == col - s, 1.0, 0.0).astype(BF16)[:, : min(LANES, width - s)]
        for s in range(0, width, LANES)
    ]
    return jnp.concatenate(parts, axis=1)


def pick_sublanes(row, start, height):
    ids = lax.broadcasted_iota(jnp.int32, (height, row.shape[1]), 0)
    return jnp.where(ids == row - start, 1.0, 0.0).astype(BF16)


def fold_of(index, height):
    hi = jnp.zeros_like(index)
    for j in range(1, FOLDS):
        hi = hi + jnp.where(index >= j * height, 1, 0)
    return hi


def gather_folded(col, table):
    height = table.shape[0]
    width = table.shape[1] // FOLDS
    hi = fold_of(col, height)
    wide = mm(pick_lanes(col - hi * height, height), table)
    out = wide[:, :width]
    for j in range(1, FOLDS):
        out = jnp.where(hi == j, wide[:, j * width : (j + 1) * width], out)
    return out


def spread_folds(values, hi):
    values = values.astype(F32)
    return jnp.concatenate(
        [jnp.where(hi == j, values, 0.0).astype(BF16) for j in range(FOLDS)], axis=1
    )


def scatter_folded(row, wide_ref, height, tile, write):
    width = wide_ref.shape[1] // FOLDS
    low = row - fold_of(row, height) * height
    for start in range(0, height, tile):
        sums = mm(pick_sublanes(low, start, tile), wide_ref[...])
        for j in range(FOLDS):
            write(j * height + start, sums[:, j * width : (j + 1) * width])


def write_folded(table, rows, latent):
    height = table.shape[0]
    for j in range(FOLDS):
        table[:, j * latent : (j + 1) * latent] = rows(j * height, height)


def forward_kernel(
    chunk, nodes_ref, ghosts_ref, send_ref, recv_ref, count_ref, pool_row_ref,
    wei_ref, weo_ref, wni_ref, wno_ref,
    fine_ref, window_ref, pre_ref, node_pre_ref, summed_ref,
    lookup, send_table, recv_table, wide,
):
    rows, latent = nodes_ref.shape
    lookup[:rows, :] = nodes_ref[...]
    lookup[rows:, :] = ghosts_ref[...]
    write_folded(send_table, lambda s, h: mm(lookup[s : s + h, :], wei_ref[:latent, :]).astype(BF16), latent)
    write_folded(recv_table, lambda s, h: mm(nodes_ref[s : s + h, :], wei_ref[latent:, :]).astype(BF16), latent)

    def edges(i, carry):
        at = pl.ds(pl.multiple_of(i * chunk, chunk), chunk)
        recv = columns(alive(recv_ref[:, at], i * chunk, count_ref[...]))
        pre = gather_folded(columns(send_ref[:, at]), send_table[...]) + gather_folded(recv, recv_table[...])
        pre_ref[at, :] = pre
        act = (pre * sigmoid(pre)).astype(BF16)
        message = mm(act, weo_ref[...]).astype(BF16)
        wide[at, :] = spread_folds(message, fold_of(recv, rows // FOLDS))
        return carry

    lax.fori_loop(0, send_ref.shape[1] // chunk, edges, 0)

    def put(s, v):
        summed_ref[s : s + v.shape[0], :] = v.astype(BF16)

    scatter_folded(alive(recv_ref[...], 0, count_ref[...]), wide, rows // FOLDS, min(256, rows // FOLDS), put)
    node_pre = mm(nodes_ref[...], wni_ref[:latent, :]) + mm(summed_ref[...], wni_ref[latent:, :])
    node_pre_ref[...] = node_pre
    node_act = (node_pre * sigmoid(node_pre)).astype(BF16)
    fine = (nodes_ref[...].astype(F32) + mm(node_act, wno_ref[...])).astype(BF16)
    fine_ref[...] = fine
    window_ref[...] = mm(pick_sublanes(pool_row_ref[...], 0, window_ref.shape[0]), fine)


def halo_pair(n_gy, low, high, got, send_sem, recv_sem):
    b = lax.axis_index("gy")
    down = pltpu.make_async_remote_copy(
        src_ref=low, dst_ref=got.at[1], send_sem=send_sem.at[0], recv_sem=recv_sem.at[1],
        device_id=(lax.axis_index("gx"), jnp.maximum(b - 1, 0)), device_id_type=MESH)
    up = pltpu.make_async_remote_copy(
        src_ref=high, dst_ref=got.at[0], send_sem=send_sem.at[1], recv_sem=recv_sem.at[0],
        device_id=(lax.axis_index("gx"), jnp.minimum(b + 1, n_gy - 1)), device_id_type=MESH)

    @pl.when(b > 0)
    def _():
        down.start()

    @pl.when(b < n_gy - 1)
    def _():
        up.start()

    @pl.when(b == 0)
    def _():
        got[0] = jnp.zeros(got.shape[1:], got.dtype)

    @pl.when(b == n_gy - 1)
    def _():
        got[1] = jnp.zeros(got.shape[1:], got.dtype)

    @pl.when(b > 0)
    def _():
        down.wait_send()
        up.wait_recv()

    @pl.when(b < n_gy - 1)
    def _():
        up.wait_send()
        down.wait_recv()


def coarse_kernel(
    n_gy, window_ref, d_coarse_ref, wci_ref, wco_ref,
    out_ref, reach_ref, g_in_ref, g_out_ref,
    rims, got_rims, bands, got_bands, send_sem, recv_sem,
):
    co = d_coarse_ref.shape[0]
    a, b = lax.axis_index("gx"), lax.axis_index("gy")
    barrier = pltpu.get_barrier_semaphore()

    @pl.when(b > 0)
    def _():
        pl.semaphore_signal(barrier, inc=1, device_id=(a, jnp.maximum(b - 1, 0)), device_id_type=MESH)

    @pl.when(b < n_gy - 1)
    def _():
        pl.semaphore_signal(barrier, inc=1, device_id=(a, jnp.minimum(b + 1, n_gy - 1)), device_id_type=MESH)

    rims[0] = window_ref[:BAND, :].astype(BF16)
    rims[1] = window_ref[co + BAND :, :].astype(BF16)

    pl.semaphore_wait(barrier, jnp.where(b > 0, 1, 0) + jnp.where(b < n_gy - 1, 1, 0))
    halo_pair(n_gy, rims.at[0], rims.at[1], got_rims, send_sem.at[0], recv_sem.at[0])
    own = window_ref[BAND : co + BAND, :]
    pooled = jnp.concatenate(
        [
            own[:BAND] + got_rims[0].astype(F32),
            own[BAND : co - BAND],
            own[co - BAND :] + got_rims[1].astype(F32),
        ],
        axis=0,
    )
    coarse_in = (0.125 * pooled).astype(BF16)
    d_coarse = d_coarse_ref[...]
    pre = mm(coarse_in, wci_ref[...])
    s = sigmoid(pre)
    d_pre = (mm_t(d_coarse, wco_ref[...]) * (s * (1.0 + pre * (1.0 - s)))).astype(BF16)
    d_in = (d_coarse.astype(F32) + mm_t(d_pre, wci_ref[...])).astype(BF16)
    bands[0] = d_in[:BAND]
    bands[1] = d_in[co - BAND :]
    reach_ref[BAND : co + BAND, :] = d_in
    halo_pair(n_gy, bands.at[0], bands.at[1], got_bands, send_sem.at[1], recv_sem.at[1])
    act = (pre * s).astype(BF16)
    out_ref[...] = (coarse_in.astype(F32) + mm(act, wco_ref[...])).astype(BF16)
    g_out_ref[...] = t_mm(act, d_coarse)
    g_in_ref[...] = t_mm(coarse_in, d_pre)
    reach_ref[:BAND, :] = got_bands[0]
    reach_ref[co + BAND :, :] = got_bands[1]


def backward_kernel(
    chunk, nodes_ref, ghosts_ref, recv_ref, count_ref, send_ref, pool_ref,
    wei_ref, weo_ref, wni_ref, wno_ref,
    pre_ref, node_pre_ref, summed_ref, reach_ref, d_fine_ref, g_ci_ref, g_co_ref,
    d_owned_ref, d_ghost_ref, g_ref,
    table, recv_wide, send_wide, sums_s, sums_r, g_out,
):
    rows, latent = nodes_ref.shape
    total_rows = rows + ghosts_ref.shape[0]
    nodes = nodes_ref[...]
    d_total = d_fine_ref[...].astype(F32) + 0.125 * mm(
        pick_lanes(columns(pool_ref[...]), reach_ref.shape[0]), reach_ref[...]
    )
    d16 = d_total.astype(BF16)
    node_pre = node_pre_ref[...]
    s = sigmoid(node_pre)
    node_act = (node_pre * s).astype(BF16)
    d_node = (mm_t(d16, wno_ref[...]) * (s * (1.0 + node_pre * (1.0 - s)))).astype(BF16)
    base = 2 * latent
    g_ref[base + latent : base + 2 * latent, :] = t_mm(nodes, d_node)
    g_ref[base + 2 * latent : base + 3 * latent, :] = t_mm(summed_ref[...], d_node)
    g_ref[base + 3 * latent : base + 4 * latent, :] = t_mm(node_act, d16)
    g_ref[base + 4 * latent : base + 5 * latent, :] = g_ci_ref[...]
    g_ref[base + 5 * latent : base + 6 * latent, :] = g_co_ref[...]
    d_owned_ref[...] = d_total + mm_t(d_node, wni_ref[:latent, :])
    d_summed = mm_t(d_node, wni_ref[latent:, :]).astype(BF16)
    height = rows // FOLDS
    for j in range(FOLDS):
        table[:, j * latent : (j + 1) * latent] = d_summed[j * height : (j + 1) * height]
    g_out[...] = jnp.zeros_like(g_out)

    def edges(i, carry):
        at = pl.ds(pl.multiple_of(i * chunk, chunk), chunk)
        recv = columns(alive(recv_ref[:, at], i * chunk, count_ref[...]))
        d_message = gather_folded(recv, table[...]).astype(BF16)
        pre = pre_ref[at, :]
        sig = sigmoid(pre)
        act = (pre * sig).astype(BF16)
        g_out[...] += t_mm(act, d_message)
        d_pre = (mm_t(d_message, weo_ref[...]) * (sig * (1.0 + pre * (1.0 - sig)))).astype(BF16)
        recv_wide[at, :] = spread_folds(d_pre, fold_of(recv, height))
        send_wide[at, :] = spread_folds(d_pre, fold_of(columns(send_ref[:, at]), total_rows // FOLDS))
        return carry

    lax.fori_loop(0, send_ref.shape[1] // chunk, edges, 0)
    g_ref[base : base + latent, :] = g_out[...]

    def put_s(at, v):
        sums_s[at : at + v.shape[0], :] = v.astype(BF16)

    def put_r(at, v):
        sums_r[at : at + v.shape[0], :] = v.astype(BF16)

    scatter_folded(alive(recv_ref[...], 0, count_ref[...]), recv_wide, height, min(256, height), put_r)
    scatter_folded(send_ref[...], send_wide, total_rows // FOLDS, min(256, total_rows // FOLDS), put_s)
    w_send, w_recv = wei_ref[:latent, :], wei_ref[latent:, :]
    d_owned_ref[...] += mm_t(sums_s[:rows, :], w_send) + mm_t(sums_r[...], w_recv)
    d_ghost_ref[...] = mm_t(sums_s[rows:, :], w_send).astype(BF16)
    g_ref[:latent, :] = t_mm(nodes, sums_s[:rows, :]) + t_mm(ghosts_ref[...], sums_s[rows:, :])
    g_ref[latent:base, :] = t_mm(nodes, sums_r[...])


def neighbours(n_gx, n_gy, sign):
    a, b = lax.axis_index("gx"), lax.axis_index("gy")
    found = []
    for dx, dy in zip(ACROSS, ALONG):
        dx, dy = sign * dx, sign * dy
        ta, tb = a + dx, b + dy
        sa, sb = a - dx, b - dy
        there = (ta >= 0) & (ta < n_gx) & (tb >= 0) & (tb < n_gy)
        here = (sa >= 0) & (sa < n_gx) & (sb >= 0) & (sb < n_gy)
        target = (jnp.clip(ta, 0, n_gx - 1), jnp.clip(tb, 0, n_gy - 1))
        found.append((target, there, here))
    return found


def greet(barrier, found):
    for target, there, _ in found:
        @pl.when(there)
        def _(target=target):
            pl.semaphore_signal(barrier, inc=1, device_id=target, device_id_type=MESH)


def greeted(barrier, found, more=0):
    count = jnp.int32(more)
    for _, there, _ in found:
        count = count + jnp.where(there, 1, 0)
    pl.semaphore_wait(barrier, count)


def exchange_copies(found, src_ref, dst_ref, send_sem, recv_sem):
    return [
        pltpu.make_async_remote_copy(
            src_ref=src_ref.at[k], dst_ref=dst_ref.at[k], send_sem=send_sem.at[k],
            recv_sem=recv_sem.at[k], device_id=found[k][0], device_id_type=MESH)
        for k in range(len(found))
    ]


def exchange_start(found, copies, dst_ref):
    for k in range(len(found)):
        @pl.when(found[k][1])
        def _(k=k):
            copies[k].start()

    for k in range(len(found)):
        @pl.when(jnp.logical_not(found[k][2]))
        def _(k=k):
            dst_ref[k] = jnp.zeros(dst_ref.shape[1:], dst_ref.dtype)


def exchange_wait(found, copies):
    for k in range(len(found)):
        @pl.when(found[k][1])
        def _(k=k):
            copies[k].wait_send()

        @pl.when(found[k][2])
        def _(k=k):
            copies[k].wait_recv()


def ghost_row(rows_ref, count_ref, k):
    return alive(rows_ref[0, k : k + 1, :], 0, count_ref[:, k : k + 1])


def exchange_kernel(n_gx, n_gy, nodes_ref, rows_ref, count_ref, dst_ref, table, outgoing, send_sem, recv_sem):
    found = neighbours(n_gx, n_gy, 1)
    barrier = pltpu.get_barrier_semaphore()
    greet(barrier, found)
    write_folded(table, lambda s, h: nodes_ref[s : s + h, :], nodes_ref.shape[1])
    copies = exchange_copies(found, outgoing, dst_ref, send_sem, recv_sem)
    for n, k in enumerate(SEND_ORDER):
        outgoing[k] = gather_folded(columns(ghost_row(rows_ref, count_ref, k)), table[...]).astype(BF16)
        if n == 0:
            greeted(barrier, found)

        @pl.when(found[k][1])
        def _(k=k):
            copies[k].start()

    for k in range(len(found)):
        @pl.when(jnp.logical_not(found[k][2]))
        def _(k=k):
            dst_ref[k] = jnp.zeros(dst_ref.shape[1:], dst_ref.dtype)

    exchange_wait(found, copies)


def reduce_kernel(
    n_gx, n_gy, ghost_ref, g_ref, back_ref, total_ref,
    g16, got_x, mid, got_y, ghost_send, ghost_recv, xs, xr, ys, yr, xs2, xr2, ys2, yr2,
):
    a, b = lax.axis_index("gx"), lax.axis_index("gy")
    found = neighbours(n_gx, n_gy, -1)
    peers_x = [(lax.rem(a + r, n_gx), b) for r in range(1, n_gx)]
    peers_y = [(a, lax.rem(b + r, n_gy)) for r in range(1, n_gy)]
    barrier = pltpu.get_barrier_semaphore()
    corners = [f for f, dx, dy in zip(found, ACROSS, ALONG) if dx and dy]
    greet(barrier, corners)
    for peer in peers_x + peers_y:
        pl.semaphore_signal(barrier, inc=1, device_id=peer, device_id_type=MESH)
    g16[...] = g_ref[...].astype(BF16)
    greeted(barrier, corners, n_gx + n_gy - 2)

    def remote(src, dst, send, recv, peer):
        return pltpu.make_async_remote_copy(
            src_ref=src, dst_ref=dst, send_sem=send, recv_sem=recv, device_id=peer, device_id_type=MESH)

    first = [
        remote(g16.at[p[0]], got_x.at[r], xs.at[r], xr.at[r], p) for r, p in enumerate(peers_x)
    ]
    for copy in first:
        copy.start()
    copies = exchange_copies(found, ghost_ref, back_ref, ghost_send, ghost_recv)
    exchange_start(found, copies, back_ref)
    total = g_ref[a]
    for r, copy in enumerate(first):
        copy.wait_recv()
        total = total + got_x[r].astype(F32)
    mid[...] = total.astype(BF16)
    second = [
        remote(mid.at[p[1]], got_y.at[r], ys.at[r], yr.at[r], p) for r, p in enumerate(peers_y)
    ]
    for copy in second:
        copy.start()
    final = mid[b].astype(F32)
    for r, copy in enumerate(second):
        copy.wait_recv()
        final = final + got_y[r].astype(F32)
    total_ref[a, b] = final.astype(BF16)
    third = [
        remote(total_ref.at[a, b], total_ref.at[a, b], ys2.at[r], yr2.at[r], p) for r, p in enumerate(peers_y)
    ]
    for copy in third:
        copy.start()
    for copy in third:
        copy.wait_recv()
    fourth = [
        remote(total_ref.at[a], total_ref.at[a], xs2.at[r], xr2.at[r], p) for r, p in enumerate(peers_x)
    ]
    for copy in fourth:
        copy.start()
    for copy in fourth:
        copy.wait_recv()
    exchange_wait(found, copies)
    for copy in first + second + third + fourth:
        copy.wait_send()


def final_kernel(
    scale, d_owned_ref, back_ref, rows_ref, count_ref, total_ref,
    nodes_out, ei_ref, eo_ref, ni_ref, no_ref, ci_ref, co_ref, wide,
):
    height = d_owned_ref.shape[0] // FOLDS
    index = [ghost_row(rows_ref, count_ref, k) for k in range(rows_ref.shape[1])]
    for k, row in enumerate(index):
        wide[k * row.shape[1] : (k + 1) * row.shape[1], :] = spread_folds(
            back_ref[k], fold_of(columns(row), height)
        )

    def put(at, v):
        nodes_out[at : at + v.shape[0], :] = d_owned_ref[at : at + v.shape[0], :] + v

    scatter_folded(jnp.concatenate(index, axis=1), wide, height, min(256, height), put)
    at = 0
    for ref in (ei_ref, eo_ref, ni_ref, no_ref, ci_ref, co_ref):
        ref[...] = total_ref[at : at + ref.shape[0], :].astype(F32) * scale
        at += ref.shape[0]


def call(kernel, outs, scratch, args, collective_id=None):
    extra = {}
    if collective_id is not None:
        extra = dict(collective_id=collective_id, has_side_effects=True)
    vmem = pl.BlockSpec(memory_space=pltpu.VMEM)
    return pl.pallas_call(
        kernel,
        out_shape=[jax.ShapeDtypeStruct(shape, kind) for shape, kind in outs],
        in_specs=[vmem] * len(args),
        out_specs=[vmem] * len(outs),
        scratch_shapes=scratch,
        compiler_params=pltpu.CompilerParams(vmem_limit_bytes=56 * 1024 * 1024, **extra),
    )(*args)


def body(
    n_gx, n_gy, nodes, ghost_rows, ghost_count, edge_send, edge_recv, edge_count, pool_map,
    w_edge_in, w_edge_out, w_node_in, w_node_out, w_coarse_in, w_coarse_out, d_fine, d_coarse,
):
    rows, latent = nodes.shape
    _, peers, slots = ghost_rows.shape
    ghosts_n = peers * slots
    edges_n = edge_send.shape[1]
    co = d_coarse.shape[0]
    chunk = 512 if edges_n % 512 == 0 else edges_n
    dma = pltpu.SemaphoreType.DMA
    edge_total = edge_count.reshape(1, 1)
    fold_rows = rows // FOLDS
    fold_all = (rows + ghosts_n) // FOLDS

    (arrived,) = call(
        functools.partial(exchange_kernel, n_gx, n_gy), [((peers, slots, latent), BF16)],
        [pltpu.VMEM((fold_rows, FOLDS * latent), BF16), pltpu.VMEM((peers, slots, latent), BF16),
         dma((peers,)), dma((peers,))], (nodes, ghost_rows, ghost_count), 0)
    ghosts = arrived.reshape(ghosts_n, latent)
    fine_out, window, pre, node_pre, summed = call(
        functools.partial(forward_kernel, chunk),
        [((rows, latent), BF16), ((co + 2 * BAND, latent), F32), ((edges_n, latent), F32),
         ((rows, latent), F32), ((rows, latent), BF16)],
        [pltpu.VMEM((rows + ghosts_n, latent), BF16), pltpu.VMEM((fold_all, FOLDS * latent), BF16),
         pltpu.VMEM((fold_rows, FOLDS * latent), BF16), pltpu.VMEM((edges_n, FOLDS * latent), BF16)],
        (nodes, ghosts, edge_send, edge_recv, edge_total, pool_map, w_edge_in, w_edge_out, w_node_in, w_node_out))
    coarse_out, reach, g_ci, g_co = call(
        functools.partial(coarse_kernel, n_gy),
        [((co, latent), BF16), ((co + 2 * BAND, latent), BF16), ((latent, latent), F32), ((latent, latent), F32)],
        [pltpu.VMEM((2, BAND, latent), BF16)] * 4 + [dma((2, 2)), dma((2, 2))],
        (window, d_coarse, w_coarse_in, w_coarse_out), 1)
    d_owned, d_ghosts, partial = call(
        functools.partial(backward_kernel, chunk),
        [((rows, latent), F32), ((ghosts_n, latent), BF16), ((8 * latent, latent), F32)],
        [pltpu.VMEM((fold_rows, FOLDS * latent), BF16), pltpu.VMEM((edges_n, FOLDS * latent), BF16),
         pltpu.VMEM((edges_n, FOLDS * latent), BF16), pltpu.VMEM((rows + ghosts_n, latent), BF16),
         pltpu.VMEM((rows, latent), BF16), pltpu.VMEM((latent, latent), F32)],
        (nodes, ghosts, edge_recv, edge_total, edge_send, pool_map, w_edge_in, w_edge_out, w_node_in,
         w_node_out, pre, node_pre, summed, reach, d_fine, g_ci, g_co))
    share = 8 * latent // (n_gx * n_gy)
    parts = (n_gx, n_gy, share, latent)
    back, total = call(
        functools.partial(reduce_kernel, n_gx, n_gy),
        [((peers, slots, latent), BF16), (parts, BF16)],
        [pltpu.VMEM(parts, BF16), pltpu.VMEM((n_gx - 1,) + parts[1:], BF16), pltpu.VMEM(parts[1:], BF16),
         pltpu.VMEM((n_gy - 1,) + parts[2:], BF16), dma((peers,)), dma((peers,))]
        + [dma((n_gx - 1,))] * 2 + [dma((n_gy - 1,))] * 2 + [dma((n_gx - 1,))] * 2 + [dma((n_gy - 1,))] * 2,
        (d_ghosts.reshape(peers, slots, latent), partial.reshape(parts)), 2)
    scale = 1.0 / (rows * n_gx * n_gy) ** 0.5
    outs = call(
        functools.partial(final_kernel, scale),
        [((rows, latent), F32), ((2 * latent, latent), F32), ((latent, latent), F32), ((2 * latent, latent), F32),
         ((latent, latent), F32), ((latent, latent), F32), ((latent, latent), F32)],
        [pltpu.VMEM((ghosts_n, FOLDS * latent), BF16)],
        (d_owned, back, ghost_rows, ghost_count, total.reshape(8 * latent, latent)))
    return (fine_out, coarse_out) + tuple(outs)


def solution(mesh):
    split = P(("gx", "gy"), None)
    return jax.shard_map(
        functools.partial(body, mesh.shape["gx"], mesh.shape["gy"]),
        mesh=mesh,
        in_specs=(split, P(("gx", "gy"), None, None), split, split, split, P(("gx", "gy")), split)
        + (P(),) * 6
        + (split, split),
        out_specs=(split, split, split) + (P(),) * 6,
        check_vma=False,
    )
```

profile of v0, /device:TPU:0, one launch (start us, length us, event | category | flops | bytes accessed | tf_op | source)
XLA Modules:
  0.0 78.2 jit_solution(6402801092975972711)
XLA Ops:
  0.6 11.6 %shard_map.214 = bf16[8,256,128]{2,1,0:T(8,128)(2,1)} custom-call(bf16[1024,128]{1,0:T(8,128)(2,1)} %nodes_ref.5, s32[1,8,256]{2,1,0:T(8,128)} %rows_ref.3, s32[1,8]{1,0:T(1,128)} %count_ref.3), custom_call_target="tpu_custom_call" | custom-call | tf_op jit(solution)/shard_map/pallas_call | solution.py:463
  12.9 13.0 %shard_map.215 = (bf16[1024,128]{1,0:T(8,128)(2,1)}, f32[192,128]{1,0:T(8,128)}, f32[4096,128]{1,0:T(8,128)}, f32[1024,128]{1,0:T(8,128)}, bf16[1024,128]{1,0:T(8,128)(2,1)}) custom-call(bf16[1024,128]{1,0:T(8,128)(2,1)} %nodes_ref.5, bf16[2048,128]{1,0:T(8,128)(2,1)} %bitcast.7, s32[1,4096]{1,0:T(1,128)} %send_ref.3, s32[1,4096]{1,0:T(1,128)} %recv_ref.3, ...), custom_call_target="tpu_custom_call" | custom-call | tf_op jit(solution)/shard_map/pallas_call | solution.py:463
  25.9 9.3 %shard_map.216 = (bf16[128,128]{1,0:T(8,128)(2,1)}, bf16[192,128]{1,0:T(8,128)(2,1)}, f32[128,128]{1,0:T(8,128)}, f32[128,128]{1,0:T(8,128)}) custom-call(f32[192,128]{1,0:T(8,128)} %get-tuple-element.31.window_ref, bf16[128,128]{1,0:T(8,128)(2,1)} %d_coarse_ref.1, bf16[128,128]{1,0:T(8,128)(2,1)} %wci_ref.1, bf16[128,128]{1,0:T(8,128)(2,1)} %wco_ref.1), custom_call_target="tpu_custom_call" | custom-call | tf_op jit(solution)/shard_map/pallas_call | solution.py:463
  35.2 15.7 %shard_map.217 = (f32[1024,128]{1,0:T(8,128)}, bf16[2048,128]{1,0:T(8,128)(2,1)}, f32[1024,128]{1,0:T(8,128)}) custom-call(bf16[1024,128]{1,0:T(8,128)(2,1)} %nodes_ref.5, bf16[2048,128]{1,0:T(8,128)(2,1)} %bitcast.8, s32[1,4096]{1,0:T(1,128)} %recv_ref.3, s32[1,1]{1,0:T(1,128)} %bitcast.6.count_ref, s32[1,4096]{1,0:T(1,128)} %send_ref.3, ...), custom_call_target="tpu_custom_call" | custom-call | tf_op jit(solution)/shard_map/pallas_call | solution.py:463
  51.0 0.0 copy-start
  51.0 23.3 %shard_map.218 = (bf16[8,256,128]{2,1,0:T(8,128)(2,1)}, bf16[8,4,32,128]{3,2,1,0:T(8,128)(2,1)}) custom-call(bf16[8,256,128]{2,1,0:T(8,128)(2,1)} %bitcast.9, f32[8,4,32,128]{3,2,1,0:T(8,128)} %bitcast.10), custom_call_target="tpu_custom_call" | custom-call | tf_op jit(solution)/shard_map/pallas_call | solution.py:463
  74.3 3.3 %shard_map.219 = (f32[1024,128]{1,0:T(8,128)}, f32[256,128]{1,0:T(8,128)}, f32[128,128]{1,0:T(8,128)}, f32[256,128]{1,0:T(8,128)}, f32[128,128]{1,0:T(8,128)}, /*index=5*/f32[128,128]{1,0:T(8,128)}, f32[128,128]{1,0:T(8,128)}) custom-call(f32[1024,128]{1,0:T(8,128)} %get-tuple-element.39.d_owned_ref, bf16[8,256,128]{2,1,0:T(8,128)(2,1)} %get-tuple-element.42.back_ref, ...), custom_call_target="tpu_custom_call" | custom-call | tf_op jit(solution)/shard_map/pallas_call | solution.py:463
  77.6 0.0 copy-done
  77.6 0.6 copy.26
Async XLA Ops:
  51.0 26.6 %copy-start = (bf16[128,128]{1,0:T(8,128)(2,1)S(1)}, bf16[128,128]{1,0:T(8,128)(2,1)}, u32[]{:S(2)}) copy-start(bf16[128,128]{1,0:T(8,128)(2,1)} %get-tuple-element.61) | copy-start | bytes 98308
where the time goes:
time: 78.4 us; the launch traced here: 78.2 us
  Pallas kernels  76.3 us (97%)
  between operations  1.32 us (2%)
    pallas_call x6, Pallas kernels, call(): pl.pallas_call(kernel, out_shape=[jax.ShapeDtypeStruct(shape, kind) for s...  76.3 us

commit v1 on v0

v1 whole, which is shorter than its diff:
```python
import functools

import jax
import jax.numpy as jnp
from jax import lax
from jax.experimental import pallas as pl
from jax.experimental.pallas import tpu as pltpu
from jax.sharding import PartitionSpec as P

BAND = 32
MESH = pl.DeviceIdType.MESH
ACROSS = (-1, -1, -1, 0, 0, 1, 1, 1)
ALONG = (-1, 0, 1, -1, 1, -1, 0, 1)
SEND_ORDER = (3, 4, 1, 6, 0, 2, 5, 7)
GHOST_ORDER = (1, 6, 3, 4, 0, 2, 5, 7)
F32 = jnp.float32
BF16 = jnp.bfloat16
FOLDS = 4
LANES = 128


def mm(a, b):
    return jnp.dot(a, b, preferred_element_type=F32)


def mm_t(a, b):
    return lax.dot_general(a, b, (((1,), (1,)), ((), ())), preferred_element_type=F32)


def t_mm(a, b):
    return lax.dot_general(a, b, (((0,), (0,)), ((), ())), preferred_element_type=F32)


def sigmoid(v):
    return 1.0 / (1.0 + jnp.exp(-v))


def columns(row):
    return jnp.concatenate(
        [
            jnp.transpose(jnp.broadcast_to(row[:, s : s + LANES], (LANES, LANES)))
            for s in range(0, row.shape[1], LANES)
        ],
        axis=0,
    )


def alive(row, start, count):
    ids = lax.broadcasted_iota(jnp.int32, row.shape, 1) + start
    return jnp.where(ids < count, row, -1)


def pick_lanes(col, width):
    ids = lax.broadcasted_iota(jnp.int32, (col.shape[0], LANES), 1)
    parts = [
        jnp.where(ids == col - s, 1.0, 0.0).astype(BF16)[:, : min(LANES, width - s)]
        for s in range(0, width, LANES)
    ]
    return jnp.concatenate(parts, axis=1)


def pick_sublanes(row, height):
    ids = lax.broadcasted_iota(jnp.int32, (height, row.shape[1]), 0)
    return jnp.where(ids == row, 1.0, 0.0).astype(BF16)


def choose(block, first, wide):
    width = wide.shape[1] // FOLDS
    out = jnp.zeros((wide.shape[0], width), F32)
    for j in range(FOLDS):
        out = jnp.where(block == first + j, wide[:, j * width : (j + 1) * width], out)
    return out


def spread(values, fold):
    values = values.astype(F32)
    return jnp.concatenate(
        [jnp.where(fold == j, values, 0.0).astype(BF16) for j in range(FOLDS)], axis=1
    )


def slope(s, v):
    return s * (1.0 + v * (1.0 - s))


def neighbours(n_gx, n_gy, sign):
    a, b = lax.axis_index("gx"), lax.axis_index("gy")
    found = []
    for dx, dy in zip(ACROSS, ALONG):
        dx, dy = sign * dx, sign * dy
        ta, tb = a + dx, b + dy
        sa, sb = a - dx, b - dy
        there = (ta >= 0) & (ta < n_gx) & (tb >= 0) & (tb < n_gy)
        here = (sa >= 0) & (sa < n_gx) & (sb >= 0) & (sb < n_gy)
        target = (jnp.clip(ta, 0, n_gx - 1), jnp.clip(tb, 0, n_gy - 1))
        found.append((target, there, here))
    return found


def remote(src, dst, send, recv, peer):
    return pltpu.make_async_remote_copy(
        src_ref=src, dst_ref=dst, send_sem=send, recv_sem=recv, device_id=peer, device_id_type=MESH)


def exchange_copies(found, src_ref, dst_ref, send_sem, recv_sem):
    return [
        remote(src_ref.at[k], dst_ref.at[k], send_sem.at[k], recv_sem.at[k], found[k][0])
        for k in range(len(found))
    ]


def clear_absent(found, dst_ref):
    for k in range(len(found)):
        @pl.when(jnp.logical_not(found[k][2]))
        def _(k=k):
            dst_ref[k] = jnp.zeros(dst_ref.shape[1:], dst_ref.dtype)


def start(found, copies, k):
    @pl.when(found[k][1])
    def _():
        copies[k].start()


def wait_recv(found, copies, k):
    @pl.when(found[k][2])
    def _():
        copies[k].wait_recv()


def wait_sends(found, copies):
    for k in range(len(found)):
        @pl.when(found[k][1])
        def _(k=k):
            copies[k].wait_send()


class Rims:
    def __init__(self, n_gy, low, high, got, send_sem, recv_sem):
        a, b = lax.axis_index("gx"), lax.axis_index("gy")
        self.below, self.above = b > 0, b < n_gy - 1
        self.down = remote(low, got.at[1], send_sem.at[0], recv_sem.at[1], (a, jnp.maximum(b - 1, 0)))
        self.up = remote(high, got.at[0], send_sem.at[1], recv_sem.at[0], (a, jnp.minimum(b + 1, n_gy - 1)))
        self.got = got

    def start(self):
        @pl.when(self.below)
        def _():
            self.down.start()

        @pl.when(self.above)
        def _():
            self.up.start()

        for slot, there in ((0, self.below), (1, self.above)):
            @pl.when(jnp.logical_not(there))
            def _(slot=slot):
                self.got[slot] = jnp.zeros(self.got.shape[1:], self.got.dtype)

    def wait(self):
        @pl.when(self.below)
        def _():
            self.up.wait_recv()

        @pl.when(self.above)
        def _():
            self.down.wait_recv()

    def drain(self):
        @pl.when(self.below)
        def _():
            self.down.wait_send()

        @pl.when(self.above)
        def _():
            self.up.wait_send()


class Total:
    def __init__(self, peers_x, peers_y, total, g16, got_x, got_y, mine, xs, xr, ys, yr, zs, zr):
        a, b = lax.axis_index("gx"), lax.axis_index("gy")
        self.n_gy = len(peers_y) + 1
        self.total, self.g16, self.got_x, self.got_y, self.mine = total, g16, got_x, got_y, mine
        self.first = [remote(g16.at[p[0]], got_x.at[r], xs.at[r], xr.at[r], p) for r, p in enumerate(peers_x)]
        self.second = [
            remote(got_y.at[0], got_y.at[r + 1], ys.at[r], yr.at[r], p) for r, p in enumerate(peers_y)
        ]
        self.third = [remote(mine, total.at[a], zs.at[r], zr.at[r], p) for r, p in enumerate(peers_x)]

    def load(self, parts):
        flat = jnp.concatenate(parts, axis=0).astype(BF16)
        share = self.g16.shape[1]
        for i in range(self.g16.shape[0]):
            self.g16[i] = flat[i * share : (i + 1) * share]
        for copy in self.first:
            copy.start()

    def across(self):
        acc = self.g16[lax.axis_index("gx")].astype(F32)
        for r, copy in enumerate(self.first):
            copy.wait_recv()
            acc = acc + self.got_x[r].astype(F32)
        self.got_y[0] = acc.astype(BF16)
        for copy in self.second:
            copy.start()

    def along(self):
        a, b = lax.axis_index("gx"), lax.axis_index("gy")
        for copy in self.second:
            copy.wait_recv()
        acc = jnp.zeros(self.mine.shape, F32)
        for y in range(self.n_gy):
            acc = acc + self.got_y[lax.rem(b - y + self.n_gy, self.n_gy)].astype(F32)
        self.mine[...] = acc.astype(BF16)
        for copy in self.third:
            copy.start()
        self.total[a] = acc.astype(BF16)

    def finish(self):
        for copy in self.third:
            copy.wait_recv()
        for copy in self.first + self.second + self.third:
            copy.wait_send()


def main_kernel(
    n_gx, n_gy, chunk,
    nodes_ref, rows_ref, gcount_ref, send_ref, recv_ref, ecount_ref, pool_ref,
    wei_ref, weo_ref, wni_ref, wno_ref, wci_ref, wco_ref, d_fine_ref, d_coarse_ref,
    fine_ref, coarse_ref, grad_ref, early_ref, late_ref,
    outgoing, arrived, back_out, back, nodes_wide, ghost_wide, ghost_block,
    srow, rrow, s_block, r_block, s_lanes, r_lanes, r_rows, s_rows, g_rows,
    pairs, act_ref, slope_ref, wide_r, wide_s, both, node_slope,
    rims, got_rims, got_dc, g_in, g_out,
    e16, e_x, e_y, e_mine, l16, l_x, l_y, l_mine,
    out_s, out_r, ret_s, ret_r, rim_s, rim_r,
    exs, exr, eys, eyr, ezs, ezr, lxs, lxr, lys, lyr, lzs, lzr,
):
    rows, latent = nodes_ref.shape
    edges_n = send_ref.shape[1]
    peers, slots = rows_ref.shape[1:]
    co = d_coarse_ref.shape[0]
    bits = slots.bit_length() - 1
    own = rows // slots
    a, b = lax.axis_index("gx"), lax.axis_index("gy")
    found = neighbours(n_gx, n_gy, 1)
    returns = neighbours(n_gx, n_gy, -1)
    peers_x = [(lax.rem(a + r, n_gx), b) for r in range(1, n_gx)]
    peers_y = [(a, lax.rem(b + r, n_gy)) for r in range(1, n_gy)]
    corners = [f for f, dx, dy in zip(found, ACROSS, ALONG) if dx and dy]

    barrier = pltpu.get_barrier_semaphore()
    expect = jnp.int32(n_gx + n_gy - 2)
    for target, there, _ in corners:
        @pl.when(there)
        def _(target=target):
            pl.semaphore_signal(barrier, inc=1, device_id=target, device_id_type=MESH)
        expect = expect + jnp.where(there, 1, 0)
    for peer in peers_x + peers_y:
        pl.semaphore_signal(barrier, inc=1, device_id=peer, device_id_type=MESH)

    sent = exchange_copies(found, outgoing, arrived, out_s, out_r)
    returned = exchange_copies(returns, back_out, back, ret_s, ret_r)
    dc_rims = Rims(n_gy, d_coarse_ref.at[:BAND], d_coarse_ref.at[co - BAND :], got_dc, rim_s.at[0], rim_r.at[0])
    pool_rims = Rims(n_gy, rims.at[0], rims.at[1], got_rims, rim_s.at[1], rim_r.at[1])
    early = Total(peers_x, peers_y, early_ref, e16, e_x, e_y, e_mine, exs, exr, eys, eyr, ezs, ezr)
    late = Total(peers_x, peers_y, late_ref, l16, l_x, l_y, l_mine, lxs, lxr, lys, lyr, lzs, lzr)

    def ghost_row(k):
        return alive(rows_ref[0, k : k + 1, :], 0, gcount_ref[:, k : k + 1])

    for j in range(own):
        nodes_wide[:, j * latent : (j + 1) * latent] = nodes_ref[j * slots : (j + 1) * slots]
    for n, k in enumerate(SEND_ORDER):
        col = columns(ghost_row(k))
        block = col >> bits
        ghost_block[k] = block
        outgoing[k] = choose(block, 0, mm(pick_lanes(col & (slots - 1), slots), nodes_wide[...])).astype(BF16)
        if n == 0:
            pl.semaphore_wait(barrier, expect)
        start(found, sent, k)
    dc_rims.start()
    clear_absent(found, arrived)
    clear_absent(returns, back)

    send = send_ref[...]
    moved = send
    for place, k in enumerate(GHOST_ORDER):
        moved = jnp.where((send >> bits) == own + k, (send & (slots - 1)) + ((own + place) << bits), moved)
    srow[...] = moved
    rrow[...] = alive(recv_ref[...], 0, ecount_ref[0])

    def first_pass(i, carry):
        at = pl.ds(pl.multiple_of(i * chunk, chunk), chunk)
        s_col, r_col = columns(srow[:, at]), columns(rrow[:, at])
        s_blk, r_blk = s_col >> bits, r_col >> bits
        s_block[at, :] = s_blk
        r_block[at, :] = r_blk
        s_hot, r_hot = pick_lanes(s_col & (slots - 1), slots), pick_lanes(r_col & (slots - 1), slots)
        s_lanes[at, :] = s_hot
        r_lanes[at, :] = r_hot
        pairs[at, :latent] = choose(s_blk, 0, mm(s_hot, nodes_wide[...])).astype(BF16)
        pairs[at, latent:] = choose(r_blk, 0, mm(r_hot, nodes_wide[...])).astype(BF16)
        return carry

    steps = edges_n // chunk
    lax.fori_loop(0, steps, first_pass, 0)

    def hot_rows(i, carry):
        at = pl.ds(pl.multiple_of(i * chunk, chunk), chunk)
        s, r = srow[:, at], rrow[:, at]
        r_rows[:, at] = pick_sublanes(r & (slots - 1), slots)
        for t in range(s_rows.shape[0]):
            s_rows[t, :, at] = pick_sublanes(
                jnp.where((s >> bits) // FOLDS == t, s & (slots - 1), -1), slots)
        return carry

    lax.fori_loop(0, steps, hot_rows, 0)
    for k in range(peers):
        g_rows[:, k * slots : (k + 1) * slots] = pick_sublanes(ghost_row(k) & (slots - 1), slots)

    def take_ghosts(group):
        for j, k in enumerate(GHOST_ORDER[group * FOLDS : (group + 1) * FOLDS]):
            wait_recv(found, sent, k)
        for j, k in enumerate(GHOST_ORDER[group * FOLDS : (group + 1) * FOLDS]):
            ghost_wide[:, j * latent : (j + 1) * latent] = arrived[k]

    take_ghosts(0)

    def second_pass(i, carry):
        at = pl.ds(pl.multiple_of(i * chunk, chunk), chunk)
        got = choose(s_block[at, :], own, mm(s_lanes[at, :], ghost_wide[...])).astype(BF16)
        pairs[at, :latent] = pairs[at, :latent] + got
        return carry

    lax.fori_loop(0, steps, second_pass, 0)
    take_ghosts(1)

    def third_pass(i, carry):
        at = pl.ds(pl.multiple_of(i * chunk, chunk), chunk)
        got = choose(s_block[at, :], own + FOLDS, mm(s_lanes[at, :], ghost_wide[...])).astype(BF16)
        pairs[at, :latent] = pairs[at, :latent] + got
        pre = mm(pairs[at, :], wei_ref[...])
        s = sigmoid(pre)
        act = (pre * s).astype(BF16)
        act_ref[at, :] = act
        slope_ref[at, :] = slope(s, pre)
        wide_r[at, :] = spread(mm(act, weo_ref[...]).astype(BF16), r_block[at, :])
        return carry

    lax.fori_loop(0, steps, third_pass, 0)

    both[:, :latent] = nodes_ref[...]
    summed = mm(r_rows[...], wide_r[...])
    for j in range(FOLDS):
        both[j * slots : (j + 1) * slots, latent:] = summed[:, j * latent : (j + 1) * latent].astype(BF16)
    node_pre = mm(both[...], wni_ref[...])
    s = sigmoid(node_pre)
    node_act = (node_pre * s).astype(BF16)
    node_slope[...] = slope(s, node_pre)
    fine = (nodes_ref[...].astype(F32) + mm(node_act, wno_ref[...])).astype(BF16)
    fine_ref[...] = fine
    window = mm(pick_sublanes(pool_ref[...], co + 2 * BAND), fine)
    rims[0] = window[: 2 * BAND].astype(BF16)
    rims[1] = window[co:].astype(BF16)
    pool_rims.start()

    dc_rims.wait()
    d_coarse = d_coarse_ref[...]
    d_wide = jnp.concatenate([got_dc[0], d_coarse, got_dc[1]], axis=0)
    d_act = mm_t(d_wide, wco_ref[...])
    pool_hot = pick_lanes(columns(pool_ref[...]), co + 2 * BAND)
    pool_rims.wait()
    coarse_in = (0.125 * jnp.concatenate(
        [
            window[: 2 * BAND] + got_rims[0].astype(F32),
            window[2 * BAND : co],
            window[co:] + got_rims[1].astype(F32),
        ],
        axis=0,
    )).astype(BF16)
    pre = mm(coarse_in, wci_ref[...])
    s = sigmoid(pre)
    d_pre = (d_act * slope(s, pre)).astype(BF16)
    reach = (d_wide.astype(F32) + mm_t(d_pre, wci_ref[...])).astype(BF16)

    d_total = d_fine_ref[...].astype(F32) + 0.125 * mm(pool_hot, reach)
    d16 = d_total.astype(BF16)
    d_node = (mm_t(d16, wno_ref[...]) * node_slope[...]).astype(BF16)
    d_summed = mm_t(d_node, wni_ref[latent:, :]).astype(BF16)
    for j in range(FOLDS):
        ghost_wide[:, j * latent : (j + 1) * latent] = d_summed[j * slots : (j + 1) * slots]
    grad_ref[...] = d_total + mm_t(d_node, wni_ref[:latent, :])
    mid = slice(BAND, co + BAND)
    act = (pre * s)[mid].astype(BF16)
    coarse_ref[...] = (coarse_in[mid].astype(F32) + mm(act, wco_ref[...])).astype(BF16)
    early.load([
        t_mm(both[...], d_node), t_mm(node_act, d16), t_mm(coarse_in[mid], d_pre[mid]), t_mm(act, d_coarse)])
    g_in[...] = jnp.zeros_like(g_in)
    g_out[...] = jnp.zeros_like(g_out)

    def back_pass(i, carry):
        at = pl.ds(pl.multiple_of(i * chunk, chunk), chunk)
        r_blk = r_block[at, :]
        d_message = choose(r_blk, 0, mm(r_lanes[at, :], ghost_wide[...])).astype(BF16)
        g_out[...] += t_mm(act_ref[at, :], d_message)
        d_edge = (mm_t(d_message, weo_ref[...]) * slope_ref[at, :]).astype(BF16)
        g_in[...] += t_mm(pairs[at, :], d_edge)
        wide_r[at, :] = spread(d_edge, r_blk)
        wide_s[at, :] = spread(d_edge, s_block[at, :] & (FOLDS - 1))
        return carry

    lax.fori_loop(0, steps, back_pass, 0)
    late.load([g_in[...], g_out[...]])
    early.across()

    w_send, w_recv = wei_ref[:latent, :], wei_ref[latent:, :]

    def give_ghosts(group):
        sums = mm(s_rows[1 + group], wide_s[...]).astype(BF16)
        for j, k in enumerate(GHOST_ORDER[group * FOLDS : (group + 1) * FOLDS]):
            back_out[k] = mm_t(sums[:, j * latent : (j + 1) * latent], w_send).astype(BF16)
            start(returns, returned, k)

    give_ghosts(1)
    give_ghosts(0)
    late.across()
    early.along()
    sums_s = mm(s_rows[0], wide_s[...]).astype(BF16)
    sums_r = mm(r_rows[...], wide_r[...]).astype(BF16)
    for j in range(FOLDS):
        at = slice(j * slots, (j + 1) * slots)
        lanes = slice(j * latent, (j + 1) * latent)
        grad_ref[at, :] += mm_t(sums_s[:, lanes], w_send) + mm_t(sums_r[:, lanes], w_recv)
    late.along()
    for k in range(peers):
        wait_recv(returns, returned, k)
        wide_s[k * slots : (k + 1) * slots, :] = spread(back[k], ghost_block[k])
    sums_g = mm(g_rows[...], wide_s[: peers * slots, :])
    for j in range(FOLDS):
        grad_ref[j * slots : (j + 1) * slots, :] += sums_g[:, j * latent : (j + 1) * latent]
    early.finish()
    late.finish()
    wait_sends(found, sent)
    wait_sends(returns, returned)
    dc_rims.drain()
    pool_rims.drain()


def final_kernel(
    scale, fine_in, coarse_in, grad_in, early_in, late_in,
    fine_out, coarse_out, grad_out, ei_ref, eo_ref, ni_ref, no_ref, ci_ref, co_ref,
):
    fine_out[...] = fine_in[...]
    coarse_out[...] = coarse_in[...]
    grad_out[...] = grad_in[...]

    def put(total_ref, refs):
        flat = total_ref[...].reshape(-1, total_ref.shape[-1]).astype(F32) * scale
        at = 0
        for ref in refs:
            ref[...] = flat[at : at + ref.shape[0]]
            at += ref.shape[0]

    put(early_in, (ni_ref, no_ref, ci_ref, co_ref))
    put(late_in, (ei_ref, eo_ref))


def body(
    n_gx, n_gy, nodes, ghost_rows, ghost_count, edge_send, edge_recv, edge_count, pool_map,
    w_edge_in, w_edge_out, w_node_in, w_node_out, w_coarse_in, w_coarse_out, d_fine, d_coarse,
):
    rows, latent = nodes.shape
    _, peers, slots = ghost_rows.shape
    edges_n = edge_send.shape[1]
    co = d_coarse.shape[0]
    chunk = 512 if edges_n % 512 == 0 else edges_n
    groups = (rows // slots + peers) // FOLDS
    dma = pltpu.SemaphoreType.DMA
    vmem = pl.BlockSpec(memory_space=pltpu.VMEM)
    smem = pl.BlockSpec(memory_space=pltpu.SMEM)
    early_rows, late_rows = 5 * latent // n_gx, 3 * latent // n_gx

    def total_buffers(share):
        return [
            pltpu.VMEM((n_gx, share, latent), BF16), pltpu.VMEM((n_gx - 1, share, latent), BF16),
            pltpu.VMEM((n_gy, share, latent), BF16), pltpu.VMEM((share, latent), BF16)]

    total_sems = [dma((n_gx - 1,))] * 2 + [dma((n_gy - 1,))] * 2 + [dma((n_gx - 1,))] * 2
    halo = pltpu.VMEM((peers, slots, latent), BF16)
    results = pl.pallas_call(
        functools.partial(main_kernel, n_gx, n_gy, chunk),
        out_shape=[
            jax.ShapeDtypeStruct((rows, latent), BF16), jax.ShapeDtypeStruct((co, latent), BF16),
            jax.ShapeDtypeStruct((rows, latent), F32),
            jax.ShapeDtypeStruct((n_gx, early_rows, latent), BF16),
            jax.ShapeDtypeStruct((n_gx, late_rows, latent), BF16)],
        in_specs=[vmem] * 5 + [smem] + [vmem] * 9,
        out_specs=[vmem] * 5,
        scratch_shapes=[halo] * 4 + [
            pltpu.VMEM((slots, FOLDS * latent), BF16), pltpu.VMEM((slots, FOLDS * latent), BF16),
            pltpu.VMEM((peers, slots, LANES), jnp.int32),
            pltpu.VMEM((1, edges_n), jnp.int32), pltpu.VMEM((1, edges_n), jnp.int32),
            pltpu.VMEM((edges_n, LANES), jnp.int32), pltpu.VMEM((edges_n, LANES), jnp.int32),
            pltpu.VMEM((edges_n, slots), BF16), pltpu.VMEM((edges_n, slots), BF16),
            pltpu.VMEM((slots, edges_n), BF16), pltpu.VMEM((groups, slots, edges_n), BF16),
            pltpu.VMEM((slots, peers * slots), BF16),
            pltpu.VMEM((edges_n, 2 * latent), BF16), pltpu.VMEM((edges_n, latent), BF16),
            pltpu.VMEM((edges_n, latent), F32),
            pltpu.VMEM((edges_n, FOLDS * latent), BF16), pltpu.VMEM((edges_n, FOLDS * latent), BF16),
            pltpu.VMEM((rows, 2 * latent), BF16), pltpu.VMEM((rows, latent), F32),
            pltpu.VMEM((2, 2 * BAND, latent), BF16), pltpu.VMEM((2, 2 * BAND, latent), BF16),
            pltpu.VMEM((2, BAND, latent), BF16),
            pltpu.VMEM((2 * latent, latent), F32), pltpu.VMEM((latent, latent), F32),
        ] + total_buffers(early_rows) + total_buffers(late_rows)
        + [dma((peers,))] * 4 + [dma((2, 2))] * 2 + total_sems * 2,
        compiler_params=pltpu.CompilerParams(
            vmem_limit_bytes=48 * 1024 * 1024, collective_id=0, has_side_effects=True),
    )(nodes, ghost_rows, ghost_count, edge_send, edge_recv, edge_count, pool_map,
      w_edge_in, w_edge_out, w_node_in, w_node_out, w_coarse_in, w_coarse_out, d_fine, d_coarse)
    scale = 1.0 / (rows * n_gx * n_gy) ** 0.5
    fine, coarse, grads, ei, eo, ni, no, ci, co_grad = pl.pallas_call(
        functools.partial(final_kernel, scale),
        out_shape=[
            jax.ShapeDtypeStruct((rows, latent), BF16), jax.ShapeDtypeStruct((co, latent), BF16),
            jax.ShapeDtypeStruct((rows, latent), F32)] + [
            jax.ShapeDtypeStruct((n * latent, latent), F32) for n in (2, 1, 2, 1, 1, 1)],
        in_specs=[vmem] * 5,
        out_specs=[vmem] * 9,
        compiler_params=pltpu.CompilerParams(vmem_limit_bytes=8 * 1024 * 1024),
    )(*results)
    return fine, coarse, grads, ei, eo, ni, no, ci, co_grad


def solution(mesh):
    split = P(("gx", "gy"), None)
    return jax.shard_map(
        functools.partial(body, mesh.shape["gx"], mesh.shape["gy"]),
        mesh=mesh,
        in_specs=(split, P(("gx", "gy"), None, None), split, split, split, P(("gx", "gy")), split)
        + (P(),) * 6
        + (split, split),
        out_specs=(split, split, split) + (P(),) * 6,
        check_vma=False,
    )
```

time: 78.4 us -> 60.4 us (0.77)
  Pallas kernels: 76.3 us -> 48.1 us
  local copies, waits for them, and re-layouts: 0.62 us -> 10.2 us
    pallas_call x6 -> x2, Pallas kernels: 76.3 us -> 48.1 us  [the longest x1 46.9 us: body(): pl.pallas_call(functools.partial(main_kernel, n_gx, n_gy, chunk), out_sha...]
    unnamed x3 -> x28, local copies, waits for them, and re-layouts: 0.62 us -> 10.2 us
where the time goes in v1:
time: 60.4 us; the launch traced here: 59.6 us
  Pallas kernels  48.1 us (80%)
  local copies, waits for them, and re-layouts  10.2 us (17%)
  between operations  1.35 us (2%)
    pallas_call x1, Pallas kernels, body(): pl.pallas_call(functools.partial(main_kernel, n_gx, n_gy, chunk), out_sha...  46.9 us
    unnamed x28, local copies, waits for them, and re-layouts  10.2 us

profile of v1, /device:TPU:0, one launch (start us, length us, event | category | flops | bytes accessed | tf_op | source)
XLA Modules:
  0.0 59.6 jit_solution(13606446123300098430)
XLA Ops:
  0.6 0.0 copy-start.13
  1.3 0.0 copy-done.13
  1.3 0.0 copy-start
  1.3 0.9 %copy-done = bf16[1024,128]{1,0:T(8,128)(2,1)S(1)} copy-done((bf16[1024,128]{1,0:T(8,128)(2,1)S(1)}, bf16[1024,128]{1,0:T(8,128)(2,1)}, u32[]{:S(2)}) %copy-start) | copy-done | bytes 262168
  2.3 0.0 copy-start.1
  2.3 0.9 %copy-done.1 = bf16[1024,128]{1,0:T(8,128)(2,1)S(1)} copy-done((bf16[1024,128]{1,0:T(8,128)(2,1)S(1)}, bf16[1024,128]{1,0:T(8,128)(2,1)}, u32[]{:S(2)}) %copy-start.1) | copy-done | bytes 262168
  3.2 0.0 copy-start.2
  3.2 0.8 %copy-done.2 = bf16[256,128]{1,0:T(8,128)(2,1)S(1)} copy-done((bf16[256,128]{1,0:T(8,128)(2,1)S(1)}, bf16[256,128]{1,0:T(8,128)(2,1)}, u32[]{:S(2)}) %copy-start.2) | copy-done | bytes 65560
  4.1 0.0 copy-start.3
  4.1 0.8 %copy-done.3 = bf16[256,128]{1,0:T(8,128)(2,1)S(1)} copy-done((bf16[256,128]{1,0:T(8,128)(2,1)S(1)}, bf16[256,128]{1,0:T(8,128)(2,1)}, u32[]{:S(2)}) %copy-start.3) | copy-done | bytes 65560
  4.9 0.0 copy-start.4
  4.9 0.8 %copy-done.4 = bf16[128,128]{1,0:T(8,128)(2,1)S(1)} copy-done((bf16[128,128]{1,0:T(8,128)(2,1)S(1)}, bf16[128,128]{1,0:T(8,128)(2,1)}, u32[]{:S(2)}) %copy-start.4) | copy-done | bytes 32792
  5.7 0.0 copy-start.5
  5.7 0.8 %copy-done.5 = bf16[128,128]{1,0:T(8,128)(2,1)S(1)} copy-done((bf16[128,128]{1,0:T(8,128)(2,1)S(1)}, bf16[128,128]{1,0:T(8,128)(2,1)}, u32[]{:S(2)}) %copy-start.5) | copy-done | bytes 32792
  6.4 0.0 copy-start.6
  6.4 0.8 %copy-done.6 = bf16[128,128]{1,0:T(8,128)(2,1)S(1)} copy-done((bf16[128,128]{1,0:T(8,128)(2,1)S(1)}, bf16[128,128]{1,0:T(8,128)(2,1)}, u32[]{:S(2)}) %copy-start.6) | copy-done | bytes 32792
  7.2 0.0 copy-start.7
  7.2 0.8 %copy-done.7 = bf16[128,128]{1,0:T(8,128)(2,1)S(1)} copy-done((bf16[128,128]{1,0:T(8,128)(2,1)S(1)}, bf16[128,128]{1,0:T(8,128)(2,1)}, u32[]{:S(2)}) %copy-start.7) | copy-done | bytes 32792
  7.9 0.0 copy-start.8
  7.9 0.8 %copy-done.8 = bf16[128,128]{1,0:T(8,128)(2,1)S(1)} copy-done((bf16[128,128]{1,0:T(8,128)(2,1)S(1)}, bf16[128,128]{1,0:T(8,128)(2,1)}, u32[]{:S(2)}) %copy-start.8) | copy-done | bytes 32792
  8.7 0.0 copy-start.9
  8.7 0.7 %copy-done.9 = s32[1,4096]{1,0:T(1,128)S(1)} copy-done((s32[1,4096]{1,0:T(1,128)S(1)}, s32[1,4096]{1,0:T(1,128)}, u32[]{:S(2)}) %copy-start.9) | copy-done | bytes 16408
  9.4 0.0 copy-start.10
  9.4 0.7 %copy-done.10 = s32[1,4096]{1,0:T(1,128)S(1)} copy-done((s32[1,4096]{1,0:T(1,128)S(1)}, s32[1,4096]{1,0:T(1,128)}, u32[]{:S(2)}) %copy-start.10) | copy-done | bytes 16408
  10.1 0.0 copy-start.11
  10.1 0.7 %copy-done.11 = s32[1,8,256]{2,1,0:T(8,128)S(1)} copy-done((s32[1,8,256]{2,1,0:T(8,128)S(1)}, s32[1,8,256]{2,1,0:T(8,128)}, u32[]{:S(2)}) %copy-start.11) | copy-done | bytes 8216
  10.8 0.0 copy-start.12
  10.8 0.7 %copy-done.12 = s32[1,1024]{1,0:T(1,128)S(1)} copy-done((s32[1,1024]{1,0:T(1,128)S(1)}, s32[1,1024]{1,0:T(1,128)}, u32[]{:S(2)}) %copy-start.12) | copy-done | bytes 4120
  11.5 46.9 %shard_map.214 = (bf16[1024,128]{1,0:T(8,128)(2,1)S(1)}, bf16[128,128]{1,0:T(8,128)(2,1)S(1)}, f32[1024,128]{1,0:T(8,128)S(1)}, bf16[8,80,128]{2,1,0:T(8,128)(2,1)S(1)}, bf16[8,48,128]{2,1,0:T(8,128)(2,1)S(1)}) custom-call(bf16[1024,128]{1,0:T(8,128)(2,1)S(1)} %copy-done, s32[1,8,256]{2,1,0:T(8,128)S(1)} %copy-done.11, s32[1,8]{1,0:T(1,128)S(1)} %copy-done.13, ...), custom_call_target="tpu_custom_call" | custom-call | tf_op jit(solution)/shard_map/pallas_call | solution.py:491
  58.5 1.1 %shard_map.215 = (bf16[1024,128]{1,0:T(8,128)(2,1)}, bf16[128,128]{1,0:T(8,128)(2,1)}, f32[1024,128]{1,0:T(8,128)}, f32[256,128]{1,0:T(8,128)}, f32[128,128]{1,0...) custom-call(bf16[1024,128]{1,0:T(8,128)(2,1)S(1)} %get-tuple-element.14.fine_in, ...), custom_call_target="tpu_custom_call" | custom-call | tf_op jit(solution)/shard_map/pallas_call | solution.py:522
Async XLA Ops:
  0.6 0.7 %copy-start.13 = (s32[1,8]{1,0:T(1,128)S(1)}, s32[1,8]{1,0:T(1,128)}, u32[]{:S(2)}) copy-start(s32[1,8]{1,0:T(1,128)} %gcount_ref.1) | copy-start | bytes 100
  1.3 1.0 %copy-start = (bf16[1024,128]{1,0:T(8,128)(2,1)S(1)}, bf16[1024,128]{1,0:T(8,128)(2,1)}, u32[]{:S(2)}) copy-start(bf16[1024,128]{1,0:T(8,128)(2,1)} %nodes_ref.1) | copy-start | bytes 786436
  2.3 0.9 %copy-start.1 = (bf16[1024,128]{1,0:T(8,128)(2,1)S(1)}, bf16[1024,128]{1,0:T(8,128)(2,1)}, u32[]{:S(2)}) copy-start(bf16[1024,128]{1,0:T(8,128)(2,1)} %d_fine_ref.1) | copy-start | bytes 786436
  3.2 0.8 %copy-start.2 = (bf16[256,128]{1,0:T(8,128)(2,1)S(1)}, bf16[256,128]{1,0:T(8,128)(2,1)}, u32[]{:S(2)}) copy-start(bf16[256,128]{1,0:T(8,128)(2,1)} %wei_ref.1) | copy-start | bytes 196612
  4.1 0.8 %copy-start.3 = (bf16[256,128]{1,0:T(8,128)(2,1)S(1)}, bf16[256,128]{1,0:T(8,128)(2,1)}, u32[]{:S(2)}) copy-start(bf16[256,128]{1,0:T(8,128)(2,1)} %wni_ref.1) | copy-start | bytes 196612
  4.9 0.8 %copy-start.4 = (bf16[128,128]{1,0:T(8,128)(2,1)S(1)}, bf16[128,128]{1,0:T(8,128)(2,1)}, u32[]{:S(2)}) copy-start(bf16[128,128]{1,0:T(8,128)(2,1)} %weo_ref.1) | copy-start | bytes 98308
  5.7 0.8 %copy-start.5 = (bf16[128,128]{1,0:T(8,128)(2,1)S(1)}, bf16[128,128]{1,0:T(8,128)(2,1)}, u32[]{:S(2)}) copy-start(bf16[128,128]{1,0:T(8,128)(2,1)} %wno_ref.1) | copy-start | bytes 98308
  6.4 0.8 %copy-start.6 = (bf16[128,128]{1,0:T(8,128)(2,1)S(1)}, bf16[128,128]{1,0:T(8,128)(2,1)}, u32[]{:S(2)}) copy-start(bf16[128,128]{1,0:T(8,128)(2,1)} %wci_ref.1) | copy-start | bytes 98308
  7.2 0.8 %copy-start.7 = (bf16[128,128]{1,0:T(8,128)(2,1)S(1)}, bf16[128,128]{1,0:T(8,128)(2,1)}, u32[]{:S(2)}) copy-start(bf16[128,128]{1,0:T(8,128)(2,1)} %wco_ref.1) | copy-start | bytes 98308
  7.9 0.8 %copy-start.8 = (bf16[128,128]{1,0:T(8,128)(2,1)S(1)}, bf16[128,128]{1,0:T(8,128)(2,1)}, u32[]{:S(2)}) copy-start(bf16[128,128]{1,0:T(8,128)(2,1)} %d_coarse_ref.1) | copy-start | bytes 98308
  8.7 0.7 %copy-start.9 = (s32[1,4096]{1,0:T(1,128)S(1)}, s32[1,4096]{1,0:T(1,128)}, u32[]{:S(2)}) copy-start(s32[1,4096]{1,0:T(1,128)} %send_ref.1) | copy-start | bytes 49156
  9.4 0.7 %copy-start.10 = (s32[1,4096]{1,0:T(1,128)S(1)}, s32[1,4096]{1,0:T(1,128)}, u32[]{:S(2)}) copy-start(s32[1,4096]{1,0:T(1,128)} %recv_ref.1) | copy-start | bytes 49156
  10.1 0.7 %copy-start.11 = (s32[1,8,256]{2,1,0:T(8,128)S(1)}, s32[1,8,256]{2,1,0:T(8,128)}, u32[]{:S(2)}) copy-start(s32[1,8,256]{2,1,0:T(8,128)} %rows_ref.1) | copy-start | bytes 24580
  10.8 0.7 %copy-start.12 = (s32[1,1024]{1,0:T(1,128)S(1)}, s32[1,1024]{1,0:T(1,128)}, u32[]{:S(2)}) copy-start(s32[1,1024]{1,0:T(1,128)} %pool_ref.1) | copy-start | bytes 12292

commit v2 on v1

--- a/solution.py
+++ b/solution.py
@@ -225,9 +225,11 @@
 
 def main_kernel(
     n_gx, n_gy, chunk,
-    nodes_ref, rows_ref, gcount_ref, send_ref, recv_ref, ecount_ref, pool_ref,
-    wei_ref, weo_ref, wni_ref, wno_ref, wci_ref, wco_ref, d_fine_ref, d_coarse_ref,
+    ecount_ref, nodes_in, rows_in, gcount_in, send_in, recv_in, pool_in,
+    wei_in, weo_in, wni_in, wno_in, wci_in, wco_in, d_fine_in, d_coarse_in,
     fine_ref, coarse_ref, grad_ref, early_ref, late_ref,
+    nodes_ref, rows_ref, gcount_ref, send_ref, recv_ref, pool_ref,
+    wei_ref, weo_ref, wni_ref, wno_ref, wci_ref, wco_ref, d_fine_ref, d_coarse_ref, load_sem,
     outgoing, arrived, back_out, back, nodes_wide, ghost_wide, ghost_block,
     srow, rrow, s_block, r_block, s_lanes, r_lanes, r_rows, s_rows, g_rows,
     pairs, act_ref, slope_ref, wide_r, wide_s, both, node_slope,
@@ -249,6 +251,15 @@
     peers_y = [(a, lax.rem(b + r, n_gy)) for r in range(1, n_gy)]
     corners = [f for f, dx, dy in zip(found, ACROSS, ALONG) if dx and dy]
 
+    loads = [
+        pltpu.make_async_copy(src, dst, load_sem.at[i])
+        for i, (src, dst) in enumerate((
+            (rows_in, rows_ref), (gcount_in, gcount_ref), (nodes_in, nodes_ref), (d_coarse_in, d_coarse_ref),
+            (send_in, send_ref), (recv_in, recv_ref), (wei_in, wei_ref), (weo_in, weo_ref), (wni_in, wni_ref),
+            (wno_in, wno_ref), (pool_in, pool_ref), (wco_in, wco_ref), (wci_in, wci_ref), (d_fine_in, d_fine_ref)))
+    ]
+    for load in loads:
+        load.start()
     barrier = pltpu.get_barrier_semaphore()
     expect = jnp.int32(n_gx + n_gy - 2)
     for target, there, _ in corners:
@@ -269,6 +280,8 @@
     def ghost_row(k):
         return alive(rows_ref[0, k : k + 1, :], 0, gcount_ref[:, k : k + 1])
 
+    for load in loads[:3]:
+        load.wait()
     for j in range(own):
         nodes_wide[:, j * latent : (j + 1) * latent] = nodes_ref[j * slots : (j + 1) * slots]
     for n, k in enumerate(SEND_ORDER):
@@ -279,6 +292,8 @@
         if n == 0:
             pl.semaphore_wait(barrier, expect)
         start(found, sent, k)
+    for load in loads[3:]:
+        load.wait()
     dc_rims.start()
     clear_absent(found, arrived)
     clear_absent(returns, back)
@@ -474,7 +489,7 @@
     _, peers, slots = ghost_rows.shape
     edges_n = edge_send.shape[1]
     co = d_coarse.shape[0]
-    chunk = 512 if edges_n % 512 == 0 else edges_n
+    chunk = 2048 if edges_n % 2048 == 0 else edges_n
     groups = (rows // slots + peers) // FOLDS
     dma = pltpu.SemaphoreType.DMA
     vmem = pl.BlockSpec(memory_space=pltpu.VMEM)
@@ -488,6 +503,8 @@
 
     total_sems = [dma((n_gx - 1,))] * 2 + [dma((n_gy - 1,))] * 2 + [dma((n_gx - 1,))] * 2
     halo = pltpu.VMEM((peers, slots, latent), BF16)
+    arrays = (nodes, ghost_rows, ghost_count, edge_send, edge_recv, pool_map, w_edge_in, w_edge_out,
+              w_node_in, w_node_out, w_coarse_in, w_coarse_out, d_fine, d_coarse)
     results = pl.pallas_call(
         functools.partial(main_kernel, n_gx, n_gy, chunk),
         out_shape=[
@@ -495,9 +512,9 @@
             jax.ShapeDtypeStruct((rows, latent), F32),
             jax.ShapeDtypeStruct((n_gx, early_rows, latent), BF16),
             jax.ShapeDtypeStruct((n_gx, late_rows, latent), BF16)],
-        in_specs=[vmem] * 5 + [smem] + [vmem] * 9,
+        in_specs=[smem] + [pl.BlockSpec(memory_space=pltpu.HBM)] * len(arrays),
         out_specs=[vmem] * 5,
-        scratch_shapes=[halo] * 4 + [
+        scratch_shapes=[pltpu.VMEM(x.shape, x.dtype) for x in arrays] + [dma((len(arrays),))] + [halo] * 4 + [
             pltpu.VMEM((slots, FOLDS * latent), BF16), pltpu.VMEM((slots, FOLDS * latent), BF16),
             pltpu.VMEM((peers, slots, LANES), jnp.int32),
             pltpu.VMEM((1, edges_n), jnp.int32), pltpu.VMEM((1, edges_n), jnp.int32),
@@ -516,8 +533,7 @@
         + [dma((peers,))] * 4 + [dma((2, 2))] * 2 + total_sems * 2,
         compiler_params=pltpu.CompilerParams(
             vmem_limit_bytes=48 * 1024 * 1024, collective_id=0, has_side_effects=True),
-    )(nodes, ghost_rows, ghost_count, edge_send, edge_recv, edge_count, pool_map,
-      w_edge_in, w_edge_out, w_node_in, w_node_out, w_coarse_in, w_coarse_out, d_fine, d_coarse)
+    )(edge_count, *(pltpu.with_memory_space_constraint(x, pltpu.HBM) for x in arrays))
     scale = 1.0 / (rows * n_gx * n_gy) ** 0.5
     fine, coarse, grads, ei, eo, ni, no, ci, co_grad = pl.pallas_call(
         functools.partial(final_kernel, scale),

time: 60.4 us -> 43 us (0.71); the launches traced: 59.6 us -> 42.8 us
  local copies, waits for them, and re-layouts: 10.2 us -> 0 us
  Pallas kernels: 48.1 us -> 41.5 us
    unnamed x28 -> x0, local copies, waits for them, and re-layouts: 10.2 us -> none
    pallas_call x1, Pallas kernels: 46.9 us -> 40.4 us  [body(): pl.pallas_call(functools.partial(main_kernel, n_gx, n_gy, chunk), out_sha...]
where the time goes in v2:
time: 43 us; the launch traced here: 42.8 us
  Pallas kernels  41.5 us (97%)
  between operations  1.3 us (3%)
    pallas_call x1, Pallas kernels, body(): pl.pallas_call(functools.partial(main_kernel, n_gx, n_gy, chunk), out_sha...  40.4 us
    pallas_call x1, Pallas kernels, body(): pl.pallas_call(functools.partial(final_kernel, scale), out_shape=[jax.Sha...  1.14 us

profile of v2, /device:TPU:0, one launch (start us, length us, event | category | flops | bytes accessed | tf_op | source)
XLA Modules:
  0.0 42.8 jit_solution(5481147093938791211)
XLA Ops:
  1.3 40.4 %shard_map.214 = (bf16[1024,128]{1,0:T(8,128)(2,1)S(1)}, bf16[128,128]{1,0:T(8,128)(2,1)S(1)}, f32[1024,128]{1,0:T(8,128)S(1)}, bf16[8,80,128]{2,1,0:T(8,128)(2,1)S(1)}, bf16[8,48,128]{2,1,0:T(8,128)(2,1)S(1)}) custom-call(s32[1]{0:T(128)S(6)} %copy.24.ecount_ref, bf16[1024,128]{1,0:T(8,128)(2,1)} %nodes_in.1, s32[1,8,256]{2,1,0:T(8,128)} %rows_in.1, ...), custom_call_target="tpu_custom_call" | custom-call | tf_op jit(solution)/shard_map/pallas_call | solution.py:508
  41.7 1.1 %shard_map.215 = (bf16[1024,128]{1,0:T(8,128)(2,1)}, bf16[128,128]{1,0:T(8,128)(2,1)}, f32[1024,128]{1,0:T(8,128)}, f32[256,128]{1,0:T(8,128)}, f32[128,128]{1,0...) custom-call(bf16[1024,128]{1,0:T(8,128)(2,1)S(1)} %get-tuple-element.14.fine_in, ...), custom_call_target="tpu_custom_call" | custom-call | tf_op jit(solution)/shard_map/pallas_call | solution.py:538

commit v3 on v2

--- a/solution.py
+++ b/solution.py
@@ -16,6 +16,7 @@
 F32 = jnp.float32
 BF16 = jnp.bfloat16
 FOLDS = 4
+NOWHERE = 32767
 LANES = 128
 
 
@@ -32,7 +33,7 @@
 
 
 def sigmoid(v):
-    return 1.0 / (1.0 + jnp.exp(-v))
+    return 0.5 * jnp.tanh(0.5 * v) + 0.5
 
 
 def columns(row):
@@ -50,33 +51,39 @@
     return jnp.where(ids < count, row, -1)
 
 
-def pick_lanes(col, width):
-    ids = lax.broadcasted_iota(jnp.int32, (col.shape[0], LANES), 1)
+def hot(ids, index):
+    return jnp.where(ids == index, jnp.ones((), BF16), jnp.zeros((), BF16))
+
+
+def pick_lanes(col, first, width):
+    ids = lax.broadcasted_iota(jnp.int16, (col.shape[0], LANES), 1)
     parts = [
-        jnp.where(ids == col - s, 1.0, 0.0).astype(BF16)[:, : min(LANES, width - s)]
-        for s in range(0, width, LANES)
+        hot(ids + jnp.int16(first + s), col)[:, : min(LANES, width - s)] for s in range(0, width, LANES)
     ]
     return jnp.concatenate(parts, axis=1)
 
 
 def pick_sublanes(row, height):
-    ids = lax.broadcasted_iota(jnp.int32, (height, row.shape[1]), 0)
-    return jnp.where(ids == row, 1.0, 0.0).astype(BF16)
-
-
-def choose(block, first, wide):
+    return hot(lax.broadcasted_iota(jnp.int16, (height, row.shape[1]), 0), row.astype(jnp.int16))
+
+
+def choose(fold, wide):
     width = wide.shape[1] // FOLDS
-    out = jnp.zeros((wide.shape[0], width), F32)
-    for j in range(FOLDS):
-        out = jnp.where(block == first + j, wide[:, j * width : (j + 1) * width], out)
+    out = wide[:, :width]
+    for j in range(1, FOLDS):
+        out = jnp.where(fold == j, wide[:, j * width : (j + 1) * width], out)
     return out
 
 
 def spread(values, fold):
-    values = values.astype(F32)
     return jnp.concatenate(
-        [jnp.where(fold == j, values, 0.0).astype(BF16) for j in range(FOLDS)], axis=1
+        [jnp.where(fold == jnp.int16(j), values, jnp.zeros((), BF16)) for j in range(FOLDS)], axis=1
     )
+
+
+def piece(sums, j):
+    width = sums.shape[1] // FOLDS
+    return sums[:, j * width : (j + 1) * width]
 
 
 def slope(s, v):
@@ -225,15 +232,15 @@
 
 def main_kernel(
     n_gx, n_gy, chunk,
-    ecount_ref, nodes_in, rows_in, gcount_in, send_in, recv_in, pool_in,
+    ecount_in, nodes_in, rows_in, gcount_in, send_in, recv_in, pool_in,
     wei_in, weo_in, wni_in, wno_in, wci_in, wco_in, d_fine_in, d_coarse_in,
     fine_ref, coarse_ref, grad_ref, early_ref, late_ref,
-    nodes_ref, rows_ref, gcount_ref, send_ref, recv_ref, pool_ref,
+    ecount_ref, nodes_ref, rows_ref, gcount_ref, send_ref, recv_ref, pool_ref,
     wei_ref, weo_ref, wni_ref, wno_ref, wci_ref, wco_ref, d_fine_ref, d_coarse_ref, load_sem,
-    outgoing, arrived, back_out, back, nodes_wide, ghost_wide, ghost_block,
-    srow, rrow, s_block, r_block, s_lanes, r_lanes, r_rows, s_rows, g_rows,
-    pairs, act_ref, slope_ref, wide_r, wide_s, both, node_slope,
-    rims, got_rims, got_dc, g_in, g_out,
+    outgoing, arrived, back_out, back, nodes_wide, ghost_wide, ghost_fold,
+    srow, rrow, s_fold, r_fold, s_fold16, r_fold16, s_lanes, r_lanes,
+    pairs, edge16, slope_ref, wide_r, wide_s, both, agg, node_slope, d_node_ref,
+    rims, got_rims, got_dc, g_in,
     e16, e_x, e_y, e_mine, l16, l_x, l_y, l_mine,
     out_s, out_r, ret_s, ret_r, rim_s, rim_r,
     exs, exr, eys, eyr, ezs, ezr, lxs, lxr, lys, lyr, lzs, lzr,
@@ -255,7 +262,7 @@
         pltpu.make_async_copy(src, dst, load_sem.at[i])
         for i, (src, dst) in enumerate((
             (rows_in, rows_ref), (gcount_in, gcount_ref), (nodes_in, nodes_ref), (d_coarse_in, d_coarse_ref),
-            (send_in, send_ref), (recv_in, recv_ref), (wei_in, wei_ref), (weo_in, weo_ref), (wni_in, wni_ref),
+            (send_in, send_ref), (recv_in, recv_ref), (ecount_in, ecount_ref), (wei_in, wei_ref), (weo_in, weo_ref), (wni_in, wni_ref),
             (wno_in, wno_ref), (pool_in, pool_ref), (wco_in, wco_ref), (wci_in, wci_ref), (d_fine_in, d_fine_ref)))
     ]
     for load in loads:
@@ -277,6 +284,20 @@
     early = Total(peers_x, peers_y, early_ref, e16, e_x, e_y, e_mine, exs, exr, eys, eyr, ezs, ezr)
     late = Total(peers_x, peers_y, late_ref, l16, l_x, l_y, l_mine, lxs, lxr, lys, lyr, lzs, lzr)
 
+    def code(index):
+        fold = (index >> bits) & (FOLDS - 1)
+        group = jnp.where(index < 0, NOWHERE, (index >> bits) // FOLDS * slots + (index & (slots - 1)))
+        return (fold << 16) | group
+
+    def decode(row):
+        col = columns(row)
+        fold = col >> 16
+        return col.astype(jnp.int16), fold, fold.astype(jnp.int16)
+
+    def place(index, group):
+        mine = (index >= group * FOLDS * slots) & (index < (group + 1) * FOLDS * slots)
+        return jnp.where(mine, index & (slots - 1), -1)
+
     def ghost_row(k):
         return alive(rows_ref[0, k : k + 1, :], 0, gcount_ref[:, k : k + 1])
 
@@ -284,14 +305,17 @@
         load.wait()
     for j in range(own):
         nodes_wide[:, j * latent : (j + 1) * latent] = nodes_ref[j * slots : (j + 1) * slots]
-    for n, k in enumerate(SEND_ORDER):
-        col = columns(ghost_row(k))
-        block = col >> bits
-        ghost_block[k] = block
-        outgoing[k] = choose(block, 0, mm(pick_lanes(col & (slots - 1), slots), nodes_wide[...])).astype(BF16)
-        if n == 0:
+    for at in range(0, peers, FOLDS):
+        batch = SEND_ORDER[at : at + FOLDS]
+        where, fold, fold16 = decode(jnp.concatenate([code(ghost_row(k)) for k in batch], axis=1))
+        picked = choose(fold, mm(pick_lanes(where, 0, slots), nodes_wide[...])).astype(BF16)
+        for n, k in enumerate(batch):
+            ghost_fold[k] = fold16[n * slots : (n + 1) * slots]
+            outgoing[k] = picked[n * slots : (n + 1) * slots]
+        if at == 0:
             pl.semaphore_wait(barrier, expect)
-        start(found, sent, k)
+        for k in batch:
+            start(found, sent, k)
     for load in loads[3:]:
         load.wait()
     dc_rims.start()
@@ -300,39 +324,26 @@
 
     send = send_ref[...]
     moved = send
-    for place, k in enumerate(GHOST_ORDER):
-        moved = jnp.where((send >> bits) == own + k, (send & (slots - 1)) + ((own + place) << bits), moved)
+    for p, k in enumerate(GHOST_ORDER):
+        moved = jnp.where((send >> bits) == own + k, (send & (slots - 1)) + ((own + p) << bits), moved)
     srow[...] = moved
     rrow[...] = alive(recv_ref[...], 0, ecount_ref[0])
 
     def first_pass(i, carry):
         at = pl.ds(pl.multiple_of(i * chunk, chunk), chunk)
-        s_col, r_col = columns(srow[:, at]), columns(rrow[:, at])
-        s_blk, r_blk = s_col >> bits, r_col >> bits
-        s_block[at, :] = s_blk
-        r_block[at, :] = r_blk
-        s_hot, r_hot = pick_lanes(s_col & (slots - 1), slots), pick_lanes(r_col & (slots - 1), slots)
-        s_lanes[at, :] = s_hot
-        r_lanes[at, :] = r_hot
-        pairs[at, :latent] = choose(s_blk, 0, mm(s_hot, nodes_wide[...])).astype(BF16)
-        pairs[at, latent:] = choose(r_blk, 0, mm(r_hot, nodes_wide[...])).astype(BF16)
+        s_where, s_f, s_fold16[at, :] = decode(code(srow[:, at]))
+        r_where, r_f, r_fold16[at, :] = decode(code(rrow[:, at]))
+        s_fold[at, :] = s_f
+        r_fold[at, :] = r_f
+        for t in range(s_lanes.shape[0]):
+            s_lanes[t, at, :] = pick_lanes(s_where, t * slots, slots)
+        r_lanes[at, :] = pick_lanes(r_where, 0, slots)
+        pairs[at, :latent] = choose(s_f, mm(s_lanes[0, at, :], nodes_wide[...])).astype(BF16)
+        pairs[at, latent:] = choose(r_f, mm(r_lanes[at, :], nodes_wide[...])).astype(BF16)
         return carry
 
     steps = edges_n // chunk
     lax.fori_loop(0, steps, first_pass, 0)
-
-    def hot_rows(i, carry):
-        at = pl.ds(pl.multiple_of(i * chunk, chunk), chunk)
-        s, r = srow[:, at], rrow[:, at]
-        r_rows[:, at] = pick_sublanes(r & (slots - 1), slots)
-        for t in range(s_rows.shape[0]):
-            s_rows[t, :, at] = pick_sublanes(
-                jnp.where((s >> bits) // FOLDS == t, s & (slots - 1), -1), slots)
-        return carry
-
-    lax.fori_loop(0, steps, hot_rows, 0)
-    for k in range(peers):
-        g_rows[:, k * slots : (k + 1) * slots] = pick_sublanes(ghost_row(k) & (slots - 1), slots)
 
     def take_ghosts(group):
         for j, k in enumerate(GHOST_ORDER[group * FOLDS : (group + 1) * FOLDS]):
@@ -344,7 +355,7 @@
 
     def second_pass(i, carry):
         at = pl.ds(pl.multiple_of(i * chunk, chunk), chunk)
-        got = choose(s_block[at, :], own, mm(s_lanes[at, :], ghost_wide[...])).astype(BF16)
+        got = choose(s_fold[at, :], mm(s_lanes[1, at, :], ghost_wide[...])).astype(BF16)
         pairs[at, :latent] = pairs[at, :latent] + got
         return carry
 
@@ -353,22 +364,22 @@
 
     def third_pass(i, carry):
         at = pl.ds(pl.multiple_of(i * chunk, chunk), chunk)
-        got = choose(s_block[at, :], own + FOLDS, mm(s_lanes[at, :], ghost_wide[...])).astype(BF16)
+        got = choose(s_fold[at, :], mm(s_lanes[2, at, :], ghost_wide[...])).astype(BF16)
         pairs[at, :latent] = pairs[at, :latent] + got
         pre = mm(pairs[at, :], wei_ref[...])
         s = sigmoid(pre)
-        act = (pre * s).astype(BF16)
-        act_ref[at, :] = act
-        slope_ref[at, :] = slope(s, pre)
-        wide_r[at, :] = spread(mm(act, weo_ref[...]).astype(BF16), r_block[at, :])
+        act = pre * s
+        slope_ref[at, :] = s + act * (1.0 - s)
+        wide_r[at, :] = spread(act.astype(BF16), r_fold16[at, :])
         return carry
 
     lax.fori_loop(0, steps, third_pass, 0)
 
     both[:, :latent] = nodes_ref[...]
-    summed = mm(r_rows[...], wide_r[...])
+    acts = mm(pick_sublanes(place(rrow[...], 0), slots), wide_r[...]).astype(BF16)
     for j in range(FOLDS):
-        both[j * slots : (j + 1) * slots, latent:] = summed[:, j * latent : (j + 1) * latent].astype(BF16)
+        agg[j * slots : (j + 1) * slots, :] = piece(acts, j)
+    both[:, latent:] = mm(agg[...], weo_ref[...]).astype(BF16)
     node_pre = mm(both[...], wni_ref[...])
     s = sigmoid(node_pre)
     node_act = (node_pre * s).astype(BF16)
@@ -384,7 +395,7 @@
     d_coarse = d_coarse_ref[...]
     d_wide = jnp.concatenate([got_dc[0], d_coarse, got_dc[1]], axis=0)
     d_act = mm_t(d_wide, wco_ref[...])
-    pool_hot = pick_lanes(columns(pool_ref[...]), co + 2 * BAND)
+    pool_hot = pick_lanes(columns(pool_ref[...]).astype(jnp.int16), 0, co + 2 * BAND)
     pool_rims.wait()
     coarse_in = (0.125 * jnp.concatenate(
         [
@@ -403,57 +414,63 @@
     d16 = d_total.astype(BF16)
     d_node = (mm_t(d16, wno_ref[...]) * node_slope[...]).astype(BF16)
     d_summed = mm_t(d_node, wni_ref[latent:, :]).astype(BF16)
+    d_edge_out = mm_t(d_summed, weo_ref[...]).astype(BF16)
     for j in range(FOLDS):
-        ghost_wide[:, j * latent : (j + 1) * latent] = d_summed[j * slots : (j + 1) * slots]
-    grad_ref[...] = d_total + mm_t(d_node, wni_ref[:latent, :])
+        ghost_wide[:, j * latent : (j + 1) * latent] = d_edge_out[j * slots : (j + 1) * slots]
+    d_node_ref[...] = d_node
+    grad_ref[...] = d_total
     mid = slice(BAND, co + BAND)
     act = (pre * s)[mid].astype(BF16)
     coarse_ref[...] = (coarse_in[mid].astype(F32) + mm(act, wco_ref[...])).astype(BF16)
     early.load([
-        t_mm(both[...], d_node), t_mm(node_act, d16), t_mm(coarse_in[mid], d_pre[mid]), t_mm(act, d_coarse)])
+        t_mm(both[...], d_node), t_mm(node_act, d16), t_mm(coarse_in[mid], d_pre[mid]), t_mm(act, d_coarse),
+        t_mm(agg[...], d_summed)])
     g_in[...] = jnp.zeros_like(g_in)
-    g_out[...] = jnp.zeros_like(g_out)
 
     def back_pass(i, carry):
         at = pl.ds(pl.multiple_of(i * chunk, chunk), chunk)
-        r_blk = r_block[at, :]
-        d_message = choose(r_blk, 0, mm(r_lanes[at, :], ghost_wide[...])).astype(BF16)
-        g_out[...] += t_mm(act_ref[at, :], d_message)
-        d_edge = (mm_t(d_message, weo_ref[...]) * slope_ref[at, :]).astype(BF16)
+        d_act = choose(r_fold[at, :], mm(r_lanes[at, :], ghost_wide[...]))
+        d_edge = (d_act * slope_ref[at, :]).astype(BF16)
+        edge16[at, :] = d_edge
         g_in[...] += t_mm(pairs[at, :], d_edge)
-        wide_r[at, :] = spread(d_edge, r_blk)
-        wide_s[at, :] = spread(d_edge, s_block[at, :] & (FOLDS - 1))
         return carry
 
     lax.fori_loop(0, steps, back_pass, 0)
-    late.load([g_in[...], g_out[...]])
+    late.load([g_in[...]])
+    w_send, w_recv = wei_ref[:latent, :], wei_ref[latent:, :]
+    wide_s[...] = spread(edge16[...], s_fold16[...])
+
+    def send_sums(group):
+        return mm(pick_sublanes(place(srow[...], group), slots), wide_s[...]).astype(BF16)
+
+    def give_ghosts(group):
+        sums = send_sums(1 + group)
+        for j, k in enumerate(GHOST_ORDER[group * FOLDS : (group + 1) * FOLDS]):
+            back_out[k] = mm_t(piece(sums, j), w_send).astype(BF16)
+        for k in GHOST_ORDER[group * FOLDS : (group + 1) * FOLDS]:
+            start(returns, returned, k)
+
+    give_ghosts(0)
+    wide_r[...] = spread(edge16[...], r_fold16[...])
+    sums_r = mm(pick_sublanes(place(rrow[...], 0), slots), wide_r[...]).astype(BF16)
+    for j in range(FOLDS):
+        grad_ref[j * slots : (j + 1) * slots, :] += mm_t(piece(sums_r, j), w_recv)
     early.across()
-
-    w_send, w_recv = wei_ref[:latent, :], wei_ref[latent:, :]
-
-    def give_ghosts(group):
-        sums = mm(s_rows[1 + group], wide_s[...]).astype(BF16)
-        for j, k in enumerate(GHOST_ORDER[group * FOLDS : (group + 1) * FOLDS]):
-            back_out[k] = mm_t(sums[:, j * latent : (j + 1) * latent], w_send).astype(BF16)
-            start(returns, returned, k)
-
+    late.across()
     give_ghosts(1)
-    give_ghosts(0)
-    late.across()
+    sums_s = send_sums(0)
+    for j in range(FOLDS):
+        grad_ref[j * slots : (j + 1) * slots, :] += mm_t(piece(sums_s, j), w_send)
+    grad_ref[...] += mm_t(d_node_ref[...], wni_ref[:latent, :])
     early.along()
-    sums_s = mm(s_rows[0], wide_s[...]).astype(BF16)
-    sums_r = mm(r_rows[...], wide_r[...]).astype(BF16)
-    for j in range(FOLDS):
-        at = slice(j * slots, (j + 1) * slots)
-        lanes = slice(j * latent, (j + 1) * latent)
-        grad_ref[at, :] += mm_t(sums_s[:, lanes], w_send) + mm_t(sums_r[:, lanes], w_recv)
     late.along()
     for k in range(peers):
         wait_recv(returns, returned, k)
-        wide_s[k * slots : (k + 1) * slots, :] = spread(back[k], ghost_block[k])
-    sums_g = mm(g_rows[...], wide_s[: peers * slots, :])
+        wide_s[k * slots : (k + 1) * slots, :] = spread(back[k], ghost_fold[k])
+    ghosts = jnp.concatenate([place(ghost_row(k), 0) for k in range(peers)], axis=1)
+    sums_g = mm(pick_sublanes(ghosts, slots), wide_s[: peers * slots, :])
     for j in range(FOLDS):
-        grad_ref[j * slots : (j + 1) * slots, :] += sums_g[:, j * latent : (j + 1) * latent]
+        grad_ref[j * slots : (j + 1) * slots, :] += piece(sums_g, j)
     early.finish()
     late.finish()
     wait_sends(found, sent)
@@ -477,8 +494,8 @@
             ref[...] = flat[at : at + ref.shape[0]]
             at += ref.shape[0]
 
-    put(early_in, (ni_ref, no_ref, ci_ref, co_ref))
-    put(late_in, (ei_ref, eo_ref))
+    put(early_in, (ni_ref, no_ref, ci_ref, co_ref, eo_ref))
+    put(late_in, (ei_ref,))
 
 
 def body(
@@ -489,12 +506,12 @@
     _, peers, slots = ghost_rows.shape
     edges_n = edge_send.shape[1]
     co = d_coarse.shape[0]
-    chunk = 2048 if edges_n % 2048 == 0 else edges_n
+    chunk = edges_n
     groups = (rows // slots + peers) // FOLDS
     dma = pltpu.SemaphoreType.DMA
     vmem = pl.BlockSpec(memory_space=pltpu.VMEM)
-    smem = pl.BlockSpec(memory_space=pltpu.SMEM)
-    early_rows, late_rows = 5 * latent // n_gx, 3 * latent // n_gx
+    hbm = pl.BlockSpec(memory_space=pltpu.HBM)
+    early_rows, late_rows = 6 * latent // n_gx, 2 * latent // n_gx
 
     def total_buffers(share):
         return [
@@ -503,7 +520,7 @@
 
     total_sems = [dma((n_gx - 1,))] * 2 + [dma((n_gy - 1,))] * 2 + [dma((n_gx - 1,))] * 2
     halo = pltpu.VMEM((peers, slots, latent), BF16)
-    arrays = (nodes, ghost_rows, ghost_count, edge_send, edge_recv, pool_map, w_edge_in, w_edge_out,
+    arrays = (edge_count, nodes, ghost_rows, ghost_count, edge_send, edge_recv, pool_map, w_edge_in, w_edge_out,
               w_node_in, w_node_out, w_coarse_in, w_coarse_out, d_fine, d_coarse)
     results = pl.pallas_call(
         functools.partial(main_kernel, n_gx, n_gy, chunk),
@@ -512,28 +529,28 @@
             jax.ShapeDtypeStruct((rows, latent), F32),
             jax.ShapeDtypeStruct((n_gx, early_rows, latent), BF16),
             jax.ShapeDtypeStruct((n_gx, late_rows, latent), BF16)],
-        in_specs=[smem] + [pl.BlockSpec(memory_space=pltpu.HBM)] * len(arrays),
+        in_specs=[pl.BlockSpec(memory_space=pl.ANY)] + [hbm] * (len(arrays) - 1),
         out_specs=[vmem] * 5,
-        scratch_shapes=[pltpu.VMEM(x.shape, x.dtype) for x in arrays] + [dma((len(arrays),))] + [halo] * 4 + [
+        scratch_shapes=[pltpu.SMEM((1,), jnp.int32)] + [pltpu.VMEM(x.shape, x.dtype) for x in arrays[1:]] + [dma((len(arrays),))] + [halo] * 4 + [
             pltpu.VMEM((slots, FOLDS * latent), BF16), pltpu.VMEM((slots, FOLDS * latent), BF16),
-            pltpu.VMEM((peers, slots, LANES), jnp.int32),
+            pltpu.VMEM((peers, slots, LANES), jnp.int16),
             pltpu.VMEM((1, edges_n), jnp.int32), pltpu.VMEM((1, edges_n), jnp.int32),
             pltpu.VMEM((edges_n, LANES), jnp.int32), pltpu.VMEM((edges_n, LANES), jnp.int32),
-            pltpu.VMEM((edges_n, slots), BF16), pltpu.VMEM((edges_n, slots), BF16),
-            pltpu.VMEM((slots, edges_n), BF16), pltpu.VMEM((groups, slots, edges_n), BF16),
-            pltpu.VMEM((slots, peers * slots), BF16),
+            pltpu.VMEM((edges_n, LANES), jnp.int16), pltpu.VMEM((edges_n, LANES), jnp.int16),
+            pltpu.VMEM((groups, edges_n, slots), BF16), pltpu.VMEM((edges_n, slots), BF16),
             pltpu.VMEM((edges_n, 2 * latent), BF16), pltpu.VMEM((edges_n, latent), BF16),
             pltpu.VMEM((edges_n, latent), F32),
             pltpu.VMEM((edges_n, FOLDS * latent), BF16), pltpu.VMEM((edges_n, FOLDS * latent), BF16),
-            pltpu.VMEM((rows, 2 * latent), BF16), pltpu.VMEM((rows, latent), F32),
+            pltpu.VMEM((rows, 2 * latent), BF16), pltpu.VMEM((rows, latent), BF16),
+            pltpu.VMEM((rows, latent), F32), pltpu.VMEM((rows, latent), BF16),
             pltpu.VMEM((2, 2 * BAND, latent), BF16), pltpu.VMEM((2, 2 * BAND, latent), BF16),
             pltpu.VMEM((2, BAND, latent), BF16),
-            pltpu.VMEM((2 * latent, latent), F32), pltpu.VMEM((latent, latent), F32),
+            pltpu.VMEM((2 * latent, latent), F32),
         ] + total_buffers(early_rows) + total_buffers(late_rows)
         + [dma((peers,))] * 4 + [dma((2, 2))] * 2 + total_sems * 2,
         compiler_params=pltpu.CompilerParams(
             vmem_limit_bytes=48 * 1024 * 1024, collective_id=0, has_side_effects=True),
-    )(edge_count, *(pltpu.with_memory_space_constraint(x, pltpu.HBM) for x in arrays))
+    )(edge_count, *(pltpu.with_memory_space_constraint(x, pltpu.HBM) for x in arrays[1:]))
     scale = 1.0 / (rows * n_gx * n_gy) ** 0.5
     fine, coarse, grads, ei, eo, ni, no, ci, co_grad = pl.pallas_call(
         functools.partial(final_kernel, scale),

time: 43 us -> 38.8 us (0.902)
  Pallas kernels: 41.5 us -> 37.3 us
    pallas_call x1, Pallas kernels: 40.4 us -> 36.1 us  [body(): pl.pallas_call(functools.partial(main_kernel, n_gx, n_gy, chunk), out_sha...]
where the time goes in v3:
time: 38.8 us; the launch traced here: 38.6 us
  Pallas kernels  37.3 us (96%)
  between operations  1.3 us (3%)
    pallas_call x1, Pallas kernels, body(): pl.pallas_call(functools.partial(main_kernel, n_gx, n_gy, chunk), out_sha...  36.1 us
    pallas_call x1, Pallas kernels, body(): pl.pallas_call(functools.partial(final_kernel, scale), out_shape=[jax.Sha...  1.14 us

profile of v3, /device:TPU:0, one launch (start us, length us, event | category | flops | bytes accessed | tf_op | source)
XLA Modules:
  0.0 38.6 jit_solution(11702801905863271212)
XLA Ops:
  1.3 36.1 %shard_map.214 = (bf16[1024,128]{1,0:T(8,128)(2,1)S(1)}, bf16[128,128]{1,0:T(8,128)(2,1)S(1)}, f32[1024,128]{1,0:T(8,128)S(1)}, bf16[8,96,128]{2,1,0:T(8,128)(2,1)S(1)}, bf16[8,32,128]{2,1,0:T(8,128)(2,1)S(1)}) custom-call(s32[1]{0:T(128)S(6)} %copy.24.ecount_in, bf16[1024,128]{1,0:T(8,128)(2,1)} %nodes_in.1, s32[1,8,256]{2,1,0:T(8,128)} %rows_in.1, ...), custom_call_target="tpu_custom_call" | custom-call | tf_op jit(solution)/shard_map/pallas_call | solution.py:525
  37.4 1.1 %shard_map.215 = (bf16[1024,128]{1,0:T(8,128)(2,1)}, bf16[128,128]{1,0:T(8,128)(2,1)}, f32[1024,128]{1,0:T(8,128)}, f32[256,128]{1,0:T(8,128)}, f32[128,128]{1,0...) custom-call(bf16[1024,128]{1,0:T(8,128)(2,1)S(1)} %get-tuple-element.14.fine_in, ...), custom_call_target="tpu_custom_call" | custom-call | tf_op jit(solution)/shard_map/pallas_call | solution.py:555

commit v4 on v3

--- a/solution.py
+++ b/solution.py
@@ -438,39 +438,54 @@
     lax.fori_loop(0, steps, back_pass, 0)
     late.load([g_in[...]])
     w_send, w_recv = wei_ref[:latent, :], wei_ref[latent:, :]
-    wide_s[...] = spread(edge16[...], s_fold16[...])
 
     def send_sums(group):
         return mm(pick_sublanes(place(srow[...], group), slots), wide_s[...]).astype(BF16)
 
-    def give_ghosts(group):
+    def ghost_sums(group):
         sums = send_sums(1 + group)
         for j, k in enumerate(GHOST_ORDER[group * FOLDS : (group + 1) * FOLDS]):
             back_out[k] = mm_t(piece(sums, j), w_send).astype(BF16)
+
+    def give_back(group):
         for k in GHOST_ORDER[group * FOLDS : (group + 1) * FOLDS]:
             start(returns, returned, k)
 
-    give_ghosts(0)
-    wide_r[...] = spread(edge16[...], r_fold16[...])
-    sums_r = mm(pick_sublanes(place(rrow[...], 0), slots), wide_r[...]).astype(BF16)
-    for j in range(FOLDS):
-        grad_ref[j * slots : (j + 1) * slots, :] += mm_t(piece(sums_r, j), w_recv)
+    def add_sums(sums, w):
+        for j in range(FOLDS):
+            grad_ref[j * slots : (j + 1) * slots, :] += mm_t(piece(sums, j), w)
+
+    def receiver_sums():
+        wide_r[...] = spread(edge16[...], r_fold16[...])
+        add_sums(mm(pick_sublanes(place(rrow[...], 0), slots), wide_r[...]).astype(BF16), w_recv)
+
+    def own_sums():
+        add_sums(send_sums(0), w_send)
+        grad_ref[...] += mm_t(d_node_ref[...], wni_ref[:latent, :])
+
+    def add_returns(group):
+        ks = GHOST_ORDER[group * FOLDS : (group + 1) * FOLDS]
+        for n, k in enumerate(ks):
+            wait_recv(returns, returned, k)
+            wide_r[n * slots : (n + 1) * slots, :] = spread(back[k], ghost_fold[k])
+        ghosts = jnp.concatenate([place(ghost_row(k), 0) for k in ks], axis=1)
+        sums = mm(pick_sublanes(ghosts, slots), wide_r[: FOLDS * slots, :])
+        for j in range(FOLDS):
+            grad_ref[j * slots : (j + 1) * slots, :] += piece(sums, j)
+
+    wide_s[...] = spread(edge16[...], s_fold16[...])
+    ghost_sums(0)
+    give_back(0)
+    receiver_sums()
     early.across()
+    own_sums()
     late.across()
-    give_ghosts(1)
-    sums_s = send_sums(0)
-    for j in range(FOLDS):
-        grad_ref[j * slots : (j + 1) * slots, :] += mm_t(piece(sums_s, j), w_send)
-    grad_ref[...] += mm_t(d_node_ref[...], wni_ref[:latent, :])
+    ghost_sums(1)
     early.along()
+    give_back(1)
+    add_returns(0)
     late.along()
-    for k in range(peers):
-        wait_recv(returns, returned, k)
-        wide_s[k * slots : (k + 1) * slots, :] = spread(back[k], ghost_fold[k])
-    ghosts = jnp.concatenate([place(ghost_row(k), 0) for k in range(peers)], axis=1)
-    sums_g = mm(pick_sublanes(ghosts, slots), wide_s[: peers * slots, :])
-    for j in range(FOLDS):
-        grad_ref[j * slots : (j + 1) * slots, :] += piece(sums_g, j)
+    add_returns(1)
     early.finish()
     late.finish()
     wait_sends(found, sent)

time: 38.8 us -> 38.5 us (level)
  no operation moved by 1% of the time
where the time goes in v4:
time: 38.5 us; the launch traced here: 38.3 us
  Pallas kernels  37 us (96%)
  between operations  1.3 us (3%)
    pallas_call x1, Pallas kernels, body(): pl.pallas_call(functools.partial(main_kernel, n_gx, n_gy, chunk), out_sha...  35.9 us
    pallas_call x1, Pallas kernels, body(): pl.pallas_call(functools.partial(final_kernel, scale), out_shape=[jax.Sha...  1.14 us

profile of v4, /device:TPU:0, one launch (start us, length us, event | category | flops | bytes accessed | tf_op | source)
XLA Modules:
  0.0 38.3 jit_solution(9997490693139895065)
XLA Ops:
  1.3 35.9 %shard_map.214 = (bf16[1024,128]{1,0:T(8,128)(2,1)S(1)}, bf16[128,128]{1,0:T(8,128)(2,1)S(1)}, f32[1024,128]{1,0:T(8,128)S(1)}, bf16[8,96,128]{2,1,0:T(8,128)(2,1)S(1)}, bf16[8,32,128]{2,1,0:T(8,128)(2,1)S(1)}) custom-call(s32[1]{0:T(128)S(6)} %copy.24.ecount_in, bf16[1024,128]{1,0:T(8,128)(2,1)} %nodes_in.1, s32[1,8,256]{2,1,0:T(8,128)} %rows_in.1, ...), custom_call_target="tpu_custom_call" | custom-call | tf_op jit(solution)/shard_map/pallas_call | solution.py:540
  37.2 1.1 %shard_map.215 = (bf16[1024,128]{1,0:T(8,128)(2,1)}, bf16[128,128]{1,0:T(8,128)(2,1)}, f32[1024,128]{1,0:T(8,128)}, f32[256,128]{1,0:T(8,128)}, f32[128,128]{1,0...) custom-call(bf16[1024,128]{1,0:T(8,128)(2,1)S(1)} %get-tuple-element.14.fine_in, ...), custom_call_target="tpu_custom_call" | custom-call | tf_op jit(solution)/shard_map/pallas_call | solution.py:570

commit v5 on v4

--- a/solution.py
+++ b/solution.py
@@ -370,13 +370,13 @@
         s = sigmoid(pre)
         act = pre * s
         slope_ref[at, :] = s + act * (1.0 - s)
-        wide_r[at, :] = spread(act.astype(BF16), r_fold16[at, :])
+        edge16[at, :] = act.astype(BF16)
         return carry
 
     lax.fori_loop(0, steps, third_pass, 0)
 
     both[:, :latent] = nodes_ref[...]
-    acts = mm(pick_sublanes(place(rrow[...], 0), slots), wide_r[...]).astype(BF16)
+    acts = mm(pick_sublanes(place(rrow[...], 0), slots), spread(edge16[...], r_fold16[...])).astype(BF16)
     for j in range(FOLDS):
         agg[j * slots : (j + 1) * slots, :] = piece(acts, j)
     both[:, latent:] = mm(agg[...], weo_ref[...]).astype(BF16)
@@ -456,8 +456,8 @@
             grad_ref[j * slots : (j + 1) * slots, :] += mm_t(piece(sums, j), w)
 
     def receiver_sums():
-        wide_r[...] = spread(edge16[...], r_fold16[...])
-        add_sums(mm(pick_sublanes(place(rrow[...], 0), slots), wide_r[...]).astype(BF16), w_recv)
+        hits = pick_sublanes(place(rrow[...], 0), slots)
+        add_sums(mm(hits, spread(edge16[...], r_fold16[...])).astype(BF16), w_recv)
 
     def own_sums():
         add_sums(send_sums(0), w_send)

time: 38.5 us -> 38.6 us (level)
  no operation moved by 1% of the time
where the time goes in v5:
time: 38.6 us; the launch traced here: 38.4 us
  Pallas kernels  37.1 us (96%)
  between operations  1.3 us (3%)
    pallas_call x1, Pallas kernels, body(): pl.pallas_call(functools.partial(main_kernel, n_gx, n_gy, chunk), out_sha...  35.9 us
    pallas_call x1, Pallas kernels, body(): pl.pallas_call(functools.partial(final_kernel, scale), out_shape=[jax.Sha...  1.14 us

profile of v5, /device:TPU:0, one launch (start us, length us, event | category | flops | bytes accessed | tf_op | source)
XLA Modules:
  0.0 38.4 jit_solution(1865379172291462028)
XLA Ops:
  1.3 35.9 %shard_map.214 = (bf16[1024,128]{1,0:T(8,128)(2,1)S(1)}, bf16[128,128]{1,0:T(8,128)(2,1)S(1)}, f32[1024,128]{1,0:T(8,128)S(1)}, bf16[8,96,128]{2,1,0:T(8,128)(2,1)S(1)}, bf16[8,32,128]{2,1,0:T(8,128)(2,1)S(1)}) custom-call(s32[1]{0:T(128)S(6)} %copy.24.ecount_in, bf16[1024,128]{1,0:T(8,128)(2,1)} %nodes_in.1, s32[1,8,256]{2,1,0:T(8,128)} %rows_in.1, ...), custom_call_target="tpu_custom_call" | custom-call | tf_op jit(solution)/shard_map/pallas_call | solution.py:540
  37.2 1.1 %shard_map.215 = (bf16[1024,128]{1,0:T(8,128)(2,1)}, bf16[128,128]{1,0:T(8,128)(2,1)}, f32[1024,128]{1,0:T(8,128)}, f32[256,128]{1,0:T(8,128)}, f32[128,128]{1,0...) custom-call(bf16[1024,128]{1,0:T(8,128)(2,1)S(1)} %get-tuple-element.14.fine_in, ...), custom_call_target="tpu_custom_call" | custom-call | tf_op jit(solution)/shard_map/pallas_call | solution.py:570
